TPU v7x, 8 devices: a whole 2x2x1 slice. The times are simulated.
8 devices in a mesh: rep: 1 (over z), dp: 8 (over x, y, core).
Axes of the slice: x: 2, y: 2, z: 1, core: 2. Of those that a mesh axis runs over, the one named last changes fastest.
Arguments:
- x: bfloat16 [8, 2048, 896], P(('rep', 'dp'))
- dy: bfloat16 [8, 2048, 896], P(('rep', 'dp'))
- w_gate: bfloat16 [2, 896, 4864], P(None, 'dp')
- w_up: bfloat16 [2, 896, 4864], P(None, 'dp')
- w_down: bfloat16 [2, 4864, 896], P(None, 'dp')
- m_w_gate: float32 [2, 896, 4864], P(None, 'dp')
- m_w_up: float32 [2, 896, 4864], P(None, 'dp')
- m_w_down: float32 [2, 4864, 896], P(None, 'dp')
- v_w_gate: float32 [2, 896, 4864], P(None, 'dp')
- v_w_up: float32 [2, 896, 4864], P(None, 'dp')
- v_w_down: float32 [2, 4864, 896], P(None, 'dp')
Outputs:
- output 1: bfloat16 [2, 896, 4864], P('rep', 'dp')
- output 2: bfloat16 [2, 896, 4864], P('rep', 'dp')
- output 3: bfloat16 [2, 4864, 896], P('rep', 'dp')
- output 4: float32 [2, 896, 4864], P('rep', 'dp')
- output 5: float32 [2, 896, 4864], P('rep', 'dp')
- output 6: float32 [2, 4864, 896], P('rep', 'dp')
- output 7: float32 [2, 896, 4864], P('rep', 'dp')
- output 8: float32 [2, 896, 4864], P('rep', 'dp')
- output 9: float32 [2, 4864, 896], P('rep', 'dp')
All inputs are finite; a program needn't handle non-finite values.
Results may differ from a plain program's by a relative error of at most 0.0277.
Values are sent between devices in bfloat16 or wider.
A program may use at most 2 GiB of HBM per device.

v0:
```python
import jax
import jax.numpy as jnp
from jax import lax
from jax.sharding import PartitionSpec as P

NAMES = ("w_gate", "w_up", "w_down")


def matmul(a, w):
    return jnp.dot(a, w, preferred_element_type=jnp.float32).astype(jnp.bfloat16)


def normed(h):
    wide = h.astype(jnp.float32)
    scale = lax.rsqrt(jnp.mean(wide**2, -1, keepdims=True) + 1e-6)
    return (wide * scale).astype(jnp.bfloat16)


def layer(h, w):
    a = normed(h)
    gate = jnp.dot(a, w["w_gate"], preferred_element_type=jnp.float32)
    up = jnp.dot(a, w["w_up"], preferred_element_type=jnp.float32)
    return h + matmul((jax.nn.silu(gate) * up).astype(jnp.bfloat16), w["w_down"])


def adamw(w, m, v, g):
    m = 0.9 * m + 0.1 * g
    v = 0.95 * v + 0.05 * g * g
    step = m * lax.rsqrt(v + 1e-8) + 0.1 * w
    return (w - 0.02 * step).astype(jnp.bfloat16), m, v


def solution(mesh):
    def fetched(weights, number):
        return {name: lax.all_gather(w[number], "dp", axis=0, tiled=True) for name, w in zip(NAMES, weights, strict=True)}

    def step(x, dy, *arrays):
        weights, m, v = (arrays[i : i + 3] for i in (0, 3, 6))
        layers = weights[0].shape[0]
        h, kept = x[0], []
        for number in range(layers):
            kept.append(h)
            h = layer(h, fetched(weights, number))
        by_h, mine = dy[0], [None] * layers
        for number in reversed(range(layers)):
            _, back = jax.vjp(lambda w, h: layer(h, w), fetched(weights, number), kept[number])
            by_w, by_h = back(by_h)
            mine[number] = [lax.psum_scatter(by_w[name], "dp", scatter_dimension=0, tiled=True) for name in NAMES]
        gradients = [jnp.stack([mine[number][i] for number in range(layers)]).astype(jnp.float32) for i in range(3)]
        new = [adamw(w.astype(jnp.float32), m, v, g) for w, m, v, g in zip(weights, m, v, gradients, strict=True)]
        return tuple(one[which] for which in range(3) for one in new)

    states, cut = P(("rep", "dp"), None, None), P(None, "dp", None)
    return jax.shard_map(
        step,
        mesh=mesh,
        in_specs=(states, states) + (cut,) * 9,
        out_specs=(P("rep", "dp", None),) * 9,
        check_vma=False,
    )
```

profile of v0, /device:TPU:0, one launch (start us, length us, event | category | flops | bytes accessed | tf_op | source)
XLA Modules:
  0.0 879.8 jit_solution(16667950742619624621)
XLA Ops:
  7.2 0.0 all-gather.13.cloned.1.call-start
  7.2 3.2 fusion.88
  10.4 0.0 all-gather.13.cloned.1.call-update
  10.5 0.0 all-gather.15.cloned.1.call-start
  10.5 3.1 fusion.87
  13.6 0.0 all-gather.15.cloned.1.call-update
  13.6 0.0 all-gather.17.cloned.1.call-start
  13.6 1.5 fusion.86
  15.2 0.0 all-gather.17.cloned.1.call-update
  15.2 0.0 all-gather.21.cloned.1.call-start
  15.2 0.5 all-gather.21.cloned.1.call-update
  15.8 0.0 all-gather.23.cloned.1.call-start
  15.8 0.5 all-gather.23.cloned.1.call-update
  16.3 0.0 all-gather.19.cloned.1.call-start
  16.4 0.5 all-gather.19.cloned.1.call-update
  16.9 0.0 reduce-scatter.15.cloned.1.call-start
  17.0 6.1 copy.20
  23.0 2.8 fusion.36
  25.9 6.1 copy.21
  31.9 31.4 %all-gather.13.cloned.1.call-done = bf16[1,896,4864]{2,1,0:T(8,128)(2,1)} async-done(((bf16[1,112,4864]{2,1,0:T(8,128)(2,1)}), bf16[1,896,4864]{2,1,0:T(8,128)(2,1)}) %all-gather.13.cloned.1.call-update) | async-done | bytes 8716304 | tf_op jit(solution)/shard_map/all_gather | solution.py:35
  63.3 29.2 %fusion.34 = f32[2048,4864]{1,0:T(8,128)} fusion(bf16[1,896,4864]{2,1,0:T(8,128)(2,1)} %all-gather.13.cloned.1.call-done, bf16[1,2048,896]{1,2,0:T(8,128)(2,1)} %copy.20, f32[2048]{0:T(1024)S(1)} %add_rsqrt_fusion), kind=kOutput, calls=%fused_computation.52 | convolution fusion | flops 17856462848 | bytes 52240384 | tf_op jit(solution)/shard_map/dot_general | solution.py:21
  92.5 23.1 %all-gather.15.cloned.1.call-done = bf16[1,896,4864]{2,1,0:T(8,128)(2,1)} async-done(((bf16[1,112,4864]{2,1,0:T(8,128)(2,1)}), bf16[1,896,4864]{2,1,0:T(8,128)(2,1)}) %all-gather.15.cloned.1.call-update) | async-done | bytes 8716304 | tf_op jit(solution)/shard_map/all_gather | solution.py:35
  115.6 46.5 %multiply_convert_fusion.1 = (bf16[2048,4864]{1,0:T(8,128)(2,1)}, f32[2048,4864]{1,0:T(8,128)}) fusion(f32[2048,4864]{1,0:T(8,128)} %fusion.34, bf16[1,896,4864]{2,1,0:T(8,128)(2,1)} %all-gather.15.cloned.1.call-done, bf16[1,2048,896]{1,2,0:T(8,128)(2,1)} %copy.20, f32[2048]{0:T(1024)S(1)} %add_rsqrt_fusion), kind=kOutput, calls=%fused_computation.17 | convolution fusion | flops 17916231680 | bytes 112009216 | tf_op jit(solution)/shard_map/dot_general | solution.py:22
  162.2 5.8 all-gather.17.cloned.1.call-done
  168.0 25.3 %fusion.40 = (f32[2048]{0:T(1024)S(1)}, bf16[2048,896]{0,1:T(8,128)(2,1)}) fusion(bf16[2048,4864]{1,0:T(8,128)(2,1)} %get-tuple-element.24, bf16[1,4864,896]{2,1,0:T(8,128)(2,1)} %all-gather.17.cloned.1.call-done, bf16[1,2048,896]{1,2,0:T(8,128)(2,1)} %copy.20), kind=kOutput, calls=%fused_computation.58 | convolution fusion | flops 17860130816 | bytes 35987456 | tf_op jit(solution)/shard_map/dot_general | solution.py:10
  193.3 0.6 copy-done.8
  193.9 26.3 %all-gather.21.cloned.1.call-done = bf16[1,4864,896]{2,1,0:T(8,128)(2,1)} async-done(((bf16[1,608,896]{2,1,0:T(8,128)(2,1)}), bf16[1,4864,896]{2,1,0:T(8,128)(2,1)}) %all-gather.21.cloned.1.call-update) | async-done | bytes 8716304 | tf_op jit(solution)/shard_map/all_gather | solution.py:35
  220.1 28.5 %convolution_convert_fusion.1 = bf16[2048,4864]{1,0:T(8,128)(2,1)} fusion(bf16[1,4864,896]{2,1,0:T(8,128)(2,1)} %all-gather.21.cloned.1.call-done, bf16[1,2048,896]{2,1,0:T(8,128)(2,1)} %param.12), kind=kOutput, calls=%fused_computation.25 | convolution fusion | flops 17860919296 | bytes 32309248 | tf_op jit(solution)/shard_map/transpose(jvp())/dot_general | solution.py:10
  248.7 23.7 %all-gather.23.cloned.1.call-done = bf16[1,896,4864]{2,1,0:T(8,128)(2,1)} async-done(((bf16[1,112,4864]{2,1,0:T(8,128)(2,1)}), bf16[1,896,4864]{2,1,0:T(8,128)(2,1)}) %all-gather.23.cloned.1.call-update) | async-done | bytes 8716304 | tf_op jit(solution)/shard_map/all_gather | solution.py:35
  272.3 29.2 %fusion.21 = f32[2048,4864]{1,0:T(8,128)} fusion(bf16[1,896,4864]{2,1,0:T(8,128)(2,1)} %all-gather.23.cloned.1.call-done, bf16[2048,896]{0,1:T(8,128)(2,1)} %get-tuple-element.27, f32[2048]{0:T(1024)S(1)} %fusion.74), kind=kOutput, calls=%fused_computation.39 | convolution fusion | flops 17856462848 | bytes 52240384 | tf_op jit(solution)/shard_map/jvp()/dot_general | solution.py:22
  301.5 23.0 %all-gather.19.cloned.1.call-done = bf16[1,896,4864]{2,1,0:T(8,128)(2,1)} async-done(((bf16[1,112,4864]{2,1,0:T(8,128)(2,1)}), bf16[1,896,4864]{2,1,0:T(8,128)(2,1)}) %all-gather.19.cloned.1.call-update) | async-done | bytes 8716304 | tf_op jit(solution)/shard_map/all_gather | solution.py:35
  324.5 53.9 %fusion.2 = (bf16[2048,4864]{1,0:T(8,128)(2,1)}, f32[2048,4864]{1,0:T(8,128)}) fusion(f32[2048,4864]{1,0:T(8,128)} %fusion.21, bf16[2048,4864]{1,0:T(8,128)(2,1)} %convolution_convert_fusion.1, bf16[1,896,4864]{2,1,0:T(8,128)(2,1)} %all-gather.19.cloned.1.call-done, bf16[2048,896]{0,1:T(8,128)(2,1)} %get-tuple-element.27, f32[2048]{0:T(1024)S(1)} %fusion.74), kind=kOutput, calls=%fused_computation.8 | convolution fusion | flops 17976000512 | bytes 131932160 | tf_op jit(solution)/shard_map/jvp()/dot_general | solution.py:21
  378.3 29.2 %fusion.12 = bf16[2048,896]{0,1:T(8,128)(2,1)} fusion(bf16[2048,4864]{1,0:T(8,128)(2,1)} %convolution_convert_fusion.1, bf16[1,896,4864]{2,1,0:T(8,128)(2,1)} %all-gather.23.cloned.1.call-done, f32[2048,4864]{1,0:T(8,128)} %get-tuple-element.29), kind=kOutput, calls=%fused_computation.21 | convolution fusion | flops 17910726656 | bytes 72155136 | tf_op jit(solution)/shard_map/transpose(jvp())/dot_general | solution.py:22
  407.6 24.7 %fusion.42 = (f32[2048]{0:T(1024)S(1)}, bf16[2048,896]{0,1:T(8,128)(2,1)S(1)}) fusion(bf16[2048,896]{0,1:T(8,128)(2,1)S(1)} %copy-done.4, bf16[2048,896]{0,1:T(8,128)(2,1)} %fusion.12, bf16[2048,4864]{1,0:T(8,128)(2,1)} %get-tuple-element.28, bf16[1,896,4864]{2,1,0:T(8,128)(2,1)} %all-gather.19.cloned.1.call-done), kind=kOutput, calls=%fused_computation.60 | convolution fusion | flops 17860130816 | bytes 39657472 | tf_op jit(solution)/shard_map/transpose(jvp())/dot_general | solution.py:21
  432.3 2.7 fusion.59
  435.0 1.8 copy-done.5
  436.8 26.9 %convolution_convert_fusion.2 = bf16[4864,896]{1,0:T(8,128)(2,1)} fusion(bf16[2048,4864]{1,0:T(8,128)(2,1)} %get-tuple-element.24, bf16[2048,896]{0,1:T(8,128)(2,1)S(1)} %fusion.59), kind=kOutput, calls=%fused_computation.37 | convolution fusion | flops 17855315968 | bytes 32309248 | tf_op jit(solution)/shard_map/transpose(jvp())/dot_general | solution.py:10
  463.7 0.0 reduce-scatter.15.cloned.1.call-update
  463.7 0.0 reduce-scatter.17.cloned.1.call-start
  463.8 35.7 %fusion.15 = bf16[4864,896]{1,0:T(8,128)(2,1)} fusion(f32[2048,4864]{1,0:T(8,128)} %fusion.21, bf16[1,2048,896]{2,1,0:T(8,128)(2,1)} %param.12, f32[2048,4864]{1,0:T(8,128)} %get-tuple-element.29), kind=kOutput, calls=%fused_computation.33 | convolution fusion | flops 17915084800 | bytes 92078080 | tf_op jit(solution)/shard_map/transpose(jvp())/dot_general | solution.py:10
  499.5 0.0 reduce-scatter.17.cloned.1.call-update
  499.5 0.0 reduce-scatter.11.cloned.1.call-start
  499.6 27.7 %convolution_convert_fusion = bf16[2048,4864]{1,0:T(8,128)(2,1)} fusion(bf16[2048,896]{0,1:T(8,128)(2,1)} %copy-done.5, bf16[1,4864,896]{2,1,0:T(8,128)(2,1)} %all-gather.17.cloned.1.call-done), kind=kOutput, calls=%fused_computation.24 | convolution fusion | flops 17860919296 | bytes 32309248 | tf_op jit(solution)/shard_map/transpose(jvp())/dot_general | solution.py:10
  527.3 30.3 %fusion.20 = bf16[896,4864]{1,0:T(8,128)(2,1)} fusion(bf16[2048,4864]{1,0:T(8,128)(2,1)} %convolution_convert_fusion, f32[2048,4864]{1,0:T(8,128)} %fusion.34, bf16[1,2048,896]{1,2,0:T(8,128)(2,1)} %copy.20, f32[2048]{0:T(1024)S(1)} %copy-done.11), kind=kOutput, calls=%fused_computation.36 | convolution fusion | flops 17920589824 | bytes 72163328 | tf_op jit(solution)/shard_map/transpose(jvp())/dot_general | solution.py:22
  557.6 0.0 reduce-scatter.11.cloned.1.call-update
  557.6 0.0 reduce-scatter.13.cloned.1.call-start
  557.7 0.6 copy-done.7
  558.3 30.5 %fusion.16 = bf16[896,4864]{1,0:T(8,128)(2,1)} fusion(bf16[2048,4864]{1,0:T(8,128)(2,1)} %convolution_convert_fusion.1, bf16[2048,896]{0,1:T(8,128)(2,1)} %get-tuple-element.27, f32[2048]{0:T(1024)S(1)} %copy-done.7, f32[2048,4864]{1,0:T(8,128)} %get-tuple-element.29), kind=kOutput, calls=%fused_computation.34 | convolution fusion | flops 17920589824 | bytes 72163328 | tf_op jit(solution)/shard_map/transpose(jvp())/dot_general | solution.py:22
  588.8 0.0 reduce-scatter.13.cloned.1.call-update
  588.9 0.0 reduce-scatter.7.cloned.1.call-start
  588.9 38.8 %fusion.17 = bf16[896,4864]{1,0:T(8,128)(2,1)} fusion(f32[2048,4864]{1,0:T(8,128)} %fusion.34, f32[2048,4864]{1,0:T(8,128)} %get-tuple-element.25, bf16[2048,4864]{1,0:T(8,128)(2,1)} %convolution_convert_fusion, bf16[1,2048,896]{1,2,0:T(8,128)(2,1)} %copy.20, f32[2048]{0:T(1024)S(1)} %copy-done.11), kind=kOutput, calls=%fused_computation.35 | convolution fusion | flops 17970397184 | bytes 112009216 | tf_op jit(solution)/shard_map/transpose(jvp())/dot_general | solution.py:21
  627.7 0.0 reduce-scatter.9.cloned.1.call-start
  627.8 24.9 %convolution_convert_fusion.3 = bf16[896,4864]{1,0:T(8,128)(2,1)} fusion(bf16[2048,4864]{1,0:T(8,128)(2,1)} %get-tuple-element.28, bf16[2048,896]{0,1:T(8,128)(2,1)} %get-tuple-element.27, f32[2048]{0:T(1024)S(1)} %copy-done.7), kind=kOutput, calls=%fused_computation.38 | convolution fusion | flops 17856462848 | bytes 32317440 | tf_op jit(solution)/shard_map/transpose(jvp())/dot_general | solution.py:21
  652.6 0.0 reduce-scatter.9.cloned.1.call-update
  652.7 0.0 reduce-scatter.15.cloned.1.call-done
  652.7 0.0 reduce-scatter.17.cloned.1.call-done
  652.7 1.5 copy-done.2
  654.3 7.9 fusion.54
  662.1 0.6 reduce-scatter.11.cloned.1.call-done
  662.7 67.3 %reduce-scatter.13.cloned.1.call-done = bf16[112,4864]{1,0:T(8,128)(2,1)} async-done(((bf16[896,4864]{1,0:T(8,128)(2,1)}), bf16[112,4864]{1,0:T(8,128)(2,1)}) %reduce-scatter.13.cloned.1.call-update) | async-done | bytes 1089552 | tf_op jit(solution)/shard_map/reduce_scatter | solution.py:48
  730.1 8.4 fusion.50
  738.5 59.0 %reduce-scatter.7.cloned.1.call-done = bf16[112,4864]{1,0:T(8,128)(2,1)} async-done(((bf16[896,4864]{1,0:T(8,128)(2,1)}), bf16[112,4864]{1,0:T(8,128)(2,1)}) %reduce-scatter.7.cloned.1.call-update) | async-done | bytes 1089552 | tf_op jit(solution)/shard_map/reduce_scatter | solution.py:48
  797.5 67.3 %reduce-scatter.9.cloned.1.call-done = bf16[112,4864]{1,0:T(8,128)(2,1)} async-done(((bf16[896,4864]{1,0:T(8,128)(2,1)}), bf16[112,4864]{1,0:T(8,128)(2,1)}) %reduce-scatter.9.cloned.1.call-update) | async-done | bytes 1089552 | tf_op jit(solution)/shard_map/reduce_scatter | solution.py:48
  864.8 7.8 fusion.46
  (24 shorter events, 0.1 us)
Async XLA Ops:
  7.2 6.5 copy-start.1
  7.2 56.1 %all-gather.13.cloned.1.call-start = ((), (), s32[]{:S(2)}) async-start(), calls=%async_computation.12 | async-start | bytes 9805824 | tf_op jit(solution)/shard_map/all_gather | solution.py:35
  10.5 105.2 %all-gather.15.cloned.1.call-start = ((), (), s32[]{:S(2)}) async-start(), calls=%async_computation.13 | async-start | bytes 9805824 | tf_op jit(solution)/shard_map/all_gather | solution.py:35
  13.6 154.4 %all-gather.17.cloned.1.call-start = ((), (), s32[]{:S(2)}) async-start(), calls=%async_computation.14 | async-start | bytes 9805824 | tf_op jit(solution)/shard_map/all_gather | solution.py:35
  15.2 205.0 %all-gather.21.cloned.1.call-start = ((), (), s32[]{:S(2)}) async-start(), calls=%async_computation.16 | async-start | bytes 9805824 | tf_op jit(solution)/shard_map/all_gather | solution.py:35
  15.8 256.5 %all-gather.23.cloned.1.call-start = ((), (), s32[]{:S(2)}) async-start(), calls=%async_computation.17 | async-start | bytes 9805824 | tf_op jit(solution)/shard_map/all_gather | solution.py:35
  16.3 308.1 %all-gather.19.cloned.1.call-start = ((), (), s32[]{:S(2)}) async-start(), calls=%async_computation.15 | async-start | bytes 9805824 | tf_op jit(solution)/shard_map/all_gather | solution.py:35
  16.9 635.8 %reduce-scatter.15.cloned.1.call-start = ((), (), s32[]{:S(2)}) async-start(), calls=%async_computation.10 | async-start | bytes 9805824 | tf_op jit(solution)/shard_map/reduce_scatter | solution.py:48
  25.8 89.8 %copy-start.10 = (f32[2048]{0:T(1024)}, f32[2048]{0:T(1024)S(1)}, u32[]{:S(2)}) copy-start(f32[2048]{0:T(1024)S(1)} %add_rsqrt_fusion) | copy-start | bytes 24580
  193.3 0.6 copy-start.8
  193.9 238.4 %copy-start.6 = (f32[2048]{0:T(1024)}, f32[2048]{0:T(1024)S(1)}, u32[]{:S(2)}) copy-start(f32[2048]{0:T(1024)S(1)} %fusion.74) | copy-start | bytes 24580
  378.3 29.2 %copy-start.4 = (bf16[2048,896]{0,1:T(8,128)(2,1)S(1)}, bf16[2048,896]{0,1:T(8,128)(2,1)}, u32[]{:S(2)}) copy-start(bf16[2048,896]{0,1:T(8,128)(2,1)} %get-tuple-element.27) | copy-start | bytes 11010052
  407.6 24.7 %copy-start.9 = (f32[2048]{0:T(1024)S(1)}, f32[2048]{0:T(1024)}, u32[]{:S(2)}) copy-start(f32[2048]{0:T(1024)} %copy-done.8) | copy-start | bytes 24580
  407.6 24.7 %copy-start = (bf16[1,2048,896]{1,2,0:T(8,128)(2,1)S(1)}, bf16[1,2048,896]{1,2,0:T(8,128)(2,1)}, u32[]{:S(2)}) copy-start(bf16[1,2048,896]{1,2,0:T(8,128)(2,1)} %copy.21) | copy-start | bytes 11010052
  435.0 1.8 copy-start.5
  463.7 189.0 %reduce-scatter.17.cloned.1.call-start = ((), (), s32[]{:S(2)}) async-start(), calls=%async_computation.11 | async-start | bytes 9805824 | tf_op jit(solution)/shard_map/reduce_scatter | solution.py:48
  499.5 27.8 %copy-start.11 = (f32[2048]{0:T(1024)S(1)}, f32[2048]{0:T(1024)}, u32[]{:S(2)}) copy-start(f32[2048]{0:T(1024)} %copy-done.10) | copy-start | bytes 24580
  499.5 163.2 %reduce-scatter.11.cloned.1.call-start = ((), (), s32[]{:S(2)}) async-start(), calls=%async_computation.8 | async-start | bytes 9805824 | tf_op jit(solution)/shard_map/reduce_scatter | solution.py:48
  557.6 0.7 copy-start.7
  557.6 172.4 %reduce-scatter.13.cloned.1.call-start = ((), (), s32[]{:S(2)}) async-start(), calls=%async_computation.9 | async-start | bytes 9805824 | tf_op jit(solution)/shard_map/reduce_scatter | solution.py:48
  588.9 208.6 %reduce-scatter.7.cloned.1.call-start = ((), (), s32[]{:S(2)}) async-start(), calls=%async_computation.6 | async-start | bytes 9805824 | tf_op jit(solution)/shard_map/reduce_scatter | solution.py:48
  627.7 237.1 %reduce-scatter.9.cloned.1.call-start = ((), (), s32[]{:S(2)}) async-start(), calls=%async_computation.7 | async-start | bytes 9805824 | tf_op jit(solution)/shard_map/reduce_scatter | solution.py:48
  652.6 1.6 copy-start.2
  730.1 134.7 %copy-start.3 = (bf16[2,112,4864]{2,1,0:T(8,128)(2,1)S(1)}, bf16[2,112,4864]{2,1,0:T(8,128)(2,1)}, u32[]{:S(2)}) copy-start(bf16[2,112,4864]{2,1,0:T(8,128)(2,1)} %param.13) | copy-start | bytes 6537220
Sparse Core Ops, SparseCore 0:
  10.6 52.7 all-gather.12
  65.7 49.8 all-gather.14
  118.0 49.8 all-gather.16
  170.2 49.8 all-gather.20
  222.4 49.8 all-gather.22
  274.5 49.8 all-gather.18
  463.8 63.9 reduce-scatter.14
  531.3 63.9 reduce-scatter.16
  598.8 63.8 reduce-scatter.10
  666.1 63.9 reduce-scatter.12
  733.6 63.8 reduce-scatter.6
  800.8 63.9 reduce-scatter.8
where the time goes:
time: 886 us; the launch traced here: 880 us
  matrix products  481 us (54%)
  waiting for transfers between devices  329 us (37%)
  other arithmetic  29.7 us (3%)
  local copies, waits for them, and re-layouts  24.5 us (3%)
  between operations  14.6 us (2%)
    reduce_scatter x6, waiting for transfers between devices, step(): lax.psum_scatter(by_w[name], 'dp', scatter_dimension=0, tiled=True)  194 us
    dot_general x5, matrix products, layer(): gate = jnp.dot(a, w['w_gate'], preferred_element_type=jnp.float32)  171 us
    dot_general x5, matrix products, layer(): up = jnp.dot(a, w['w_up'], preferred_element_type=jnp.float32)  166 us
    dot_general x5, matrix products, matmul(): jnp.dot(a, w, preferred_element_type=jnp.float32).astype(jnp.bfloat16)  144 us
    all_gather x6, waiting for transfers between devices, fetched(): lax.all_gather(w[number], 'dp', axis=0, tiled=True)  133 us
    convert_element_type x3, other arithmetic, adamw(): return ((w - 0.02 * step).astype(jnp.bfloat16), m, v)  24.1 us
  transfers between devices with their start and end apart: 12, of which 10 were waited for; matrix products, arithmetic and copies ran while one was open for 43% of the time, Pallas kernels for 0%

commit v1 on v0

v1 whole, which is shorter than its diff:
```python
import jax
import jax.numpy as jnp
from jax import lax
from jax.experimental import pallas as pl
from jax.experimental.pallas import tpu as pltpu
from jax.sharding import PartitionSpec as P

NAMES = ("w_gate", "w_up", "w_down")
F32, BF16 = jnp.float32, jnp.bfloat16
TN = 256
ANY = pl.BlockSpec(memory_space=pl.ANY)
NT = (((1,), (1,)), ((), ()))


def dot(a, b):
    return jnp.dot(a, b, preferred_element_type=F32)


def around():
    me = lax.axis_index("dp")

    def flip(i, bit):
        return i + bit - 2 * bit * ((i // bit) % 2)

    return me, flip


def rms(h):
    wide = h.astype(F32)
    return (wide * lax.rsqrt(jnp.mean(wide * wide, -1, keepdims=True) + 1e-6)).astype(BF16)


class Piece:
    def __init__(self, shard, full, layer, rows, columns=None):
        self.shard, self.full, self.layer, self.rows, self.columns = shard, full, layer, rows, columns

    def cut(self, part):
        if self.columns is None:
            n = self.rows if part is None else self.rows // 2
            return (n if part else 0), n, slice(None)
        at, width = self.columns
        n = width if part is None else width // 2
        return 0, self.rows, pl.ds(at + (n if part else 0), n)

    def own(self):
        off, n, cols = self.cut(None)
        return self.shard.at[self.layer, pl.ds(off, n), cols]

    def there(self, owner, part=None):
        off, n, cols = self.cut(part)
        return self.full.at[self.layer, pl.ds(pl.multiple_of(owner * self.rows + off, 16), n), cols]


def forward_kernel(units, tokens, d, ff, x, dy, wg, wu, wd, WG, WU, WD, gate0, up0, p0, h1, a0T, a1T, p1, dg1, du1,
                   a_vm, dy_vm, wd_vm, own_g, own_u, own_d, send, recv, local):
    me, flip = around()
    xn, yn, pn = flip(me, 4), flip(me, 2), flip(me, 1)
    diag = flip(xn, 2)
    rg, rd = wg.shape[1], wd.shape[1]

    barrier = pltpu.get_barrier_semaphore()
    for other in (xn, yn, pn):
        pl.semaphore_signal(barrier, inc=1, device_id={"dp": other}, device_id_type=pl.DeviceIdType.MESH)
    pl.semaphore_wait(barrier, 3)

    pieces, of_unit = [], []
    for what, layer, at, width in units:
        mine = []
        if what == "g":
            mine = [Piece(wg, WG, layer, rg, (at, width)), Piece(wu, WU, layer, rg, (at, width))]
        else:
            mine = [Piece(wd, WD, layer, rd)]
        of_unit.append(range(len(pieces), len(pieces) + len(mine)))
        pieces += mine

    def go(i, kind):
        piece = pieces[i]
        src, dst, to = {
            0: (None, (me, None), xn),
            1: (None, (me, None), yn),
            2: (None, (me, None), pn),
            3: ((xn, 1), (xn, 1), yn),
            4: ((yn, 0), (yn, 0), xn),
            5: ((xn, None), (xn, None), pn),
            6: ((yn, None), (yn, None), pn),
            7: ((diag, 0), (diag, 0), pn),
            8: ((diag, 1), (diag, 1), pn),
        }[kind]
        return pltpu.make_async_remote_copy(
            src_ref=piece.own() if src is None else piece.there(*src), dst_ref=piece.there(*dst),
            send_sem=send.at[i, kind], recv_sem=recv.at[i, kind],
            device_id={"dp": to}, device_id_type=pl.DeviceIdType.MESH)

    def come(i, kind):
        owner, part, sender = {
            0: (xn, None, xn), 1: (yn, None, yn), 2: (pn, None, pn), 3: (diag, 1, yn), 4: (diag, 0, xn),
            5: (flip(pn, 4), None, pn), 6: (flip(pn, 2), None, pn), 7: (flip(diag, 1), 0, pn), 8: (flip(diag, 1), 1, pn),
        }[kind]
        ref = pieces[i].there(owner, part)
        pltpu.make_async_remote_copy(
            src_ref=ref, dst_ref=ref, send_sem=send.at[i, kind], recv_sem=recv.at[i, kind],
            device_id={"dp": sender}, device_id_type=pl.DeviceIdType.MESH).wait_recv()

    def first(u):
        for i in of_unit[u] if u < len(units) else ():
            for kind in (0, 1, 2):
                go(i, kind).start()

    def relay(u):
        for i in of_unit[u]:
            come(i, 0)
            go(i, 3).start()
            go(i, 5).start()
            come(i, 1)
            go(i, 4).start()
            go(i, 6).start()
        first(u + 2)

    def last(u):
        for i in of_unit[u]:
            come(i, 4)
            go(i, 7).start()
            come(i, 3)
            go(i, 8).start()

    def complete(u):
        for i in of_unit[u]:
            for kind in (2, 5, 6, 7, 8):
                come(i, kind)

    first(0)
    first(1)
    load = [pltpu.make_async_copy(s, t, local.at[k]) for k, (s, t) in enumerate(((x, a_vm), (dy, dy_vm), (wg, own_g), (wu, own_u), (wd, own_d)))]
    for c in load:
        c.start()
    load[0].wait()

    @pl.loop(0, tokens // TN)
    def _(i):
        rows = pl.ds(pl.multiple_of(i * TN, TN), TN)
        a_vm[rows, :] = rms(a_vm[rows, :])

    for c in load[1:]:
        c.wait()
    stores = []
    for k, (own, full, rows) in enumerate(((own_g, WG, rg), (own_u, WU, rg), (own_d, WD, rd))):
        c = pltpu.make_async_copy(own, full.at[:, pl.ds(pl.multiple_of(me * rows, 16), rows), :], local.at[5 + k])
        c.start()
        stores.append(c)

    def transpose_out(j, out):
        out[...] = a_vm[pl.ds(pl.multiple_of(j * TN, TN), TN), :].T

    def transposed(aT):
        def body(idx, out):
            transpose_out(idx.index[0], out)
        pltpu.emit_pipeline(body, grid=(tokens // TN,), out_specs=[pl.BlockSpec((d, TN), lambda j: (0, j))], _explicit_indices=True)(aT)

    TM = 512

    def gate_up(at, width):
        def body(wg_t, wu_t, gate_t, up_t, p_t):
            @pl.loop(0, tokens // TM)
            def _(i):
                rows = pl.ds(pl.multiple_of(i * TM, TM), TM)
                a = a_vm[rows, :]
                g = dot(a, wg_t[...])
                u = dot(a, wu_t[...])
                gate_t[rows, :] = g
                up_t[rows, :] = u
                p_t[rows, :] = (g * jax.nn.sigmoid(g) * u).astype(BF16)
        j0 = at // TN
        w = pl.BlockSpec((d, TN), lambda j: (0, j + j0))
        o = pl.BlockSpec((tokens, TN), lambda j: (0, j + j0))
        pltpu.emit_pipeline(body, grid=(width // TN,), in_specs=[w, w], out_specs=[o, o, o])(WG.at[0], WU.at[0], gate0, up0, p0)

    def down():
        c = pltpu.make_async_copy(WD.at[0], wd_vm, local.at[8])
        c.start()
        c.wait()

        def body(idx, p_t, x_t, h_t):
            y = dot(p_t[...], wd_vm[...]).astype(BF16)
            h = x_t[...] + y
            h_t[...] = h
            a_vm[pl.ds(pl.multiple_of(idx.index[0] * TM, TM), TM), :] = rms(h)
        o = pl.BlockSpec((TM, d), lambda i: (i, 0))
        pltpu.emit_pipeline(body, grid=(tokens // TM,), in_specs=[pl.BlockSpec((TM, ff), lambda i: (i, 0)), o], out_specs=[o], _explicit_indices=True)(p0, x, h1)

    def gate_up_back(at, width):
        def body(wg_t, wu_t, wd_t, p_t, dg_t, du_t):
            @pl.loop(0, tokens // TM)
            def _(i):
                rows = pl.ds(pl.multiple_of(i * TM, TM), TM)
                a = a_vm[rows, :]
                g = dot(a, wg_t[...])
                u = dot(a, wu_t[...])
                dp = lax.dot_general(dy_vm[rows, :], wd_t[...], NT, preferred_element_type=F32).astype(BF16).astype(F32)
                sig = jax.nn.sigmoid(g)
                s = g * sig
                p_t[rows, :] = (s * u).astype(BF16)
                du_t[rows, :] = (dp * s).astype(BF16)
                dg_t[rows, :] = (dp * u * (sig + s * (1 - sig))).astype(BF16)
        j0 = at // TN
        w = pl.BlockSpec((d, TN), lambda j: (0, j + j0))
        o = pl.BlockSpec((tokens, TN), lambda j: (0, j + j0))
        pltpu.emit_pipeline(body, grid=(width // TN,), in_specs=[w, w, pl.BlockSpec((TN, d), lambda j: (j + j0, 0))], out_specs=[o, o, o])(
            WG.at[1], WU.at[1], WD.at[1], p1, dg1, du1)

    transposed(a0T)
    for c in stores:
        c.wait()
    relay(0)
    n = len(units)
    for u, (what, layer, at, width) in enumerate(units):
        if u + 1 < n:
            relay(u + 1)
        last(u)
        complete(u)
        if what == "g" and layer == 0:
            gate_up(at, width)
        elif what == "g":
            gate_up_back(at, width)
        elif layer == 0:
            down()
            transposed(a1T)
    for i in range(len(pieces)):
        for kind in range(9):
            go(i, kind).wait_send()


def forward(x, dy, wg, wu, wd):
    tokens, d = x.shape
    ff = wg.shape[2]
    tiles = ff // TN
    a, b = (tiles + 1) // 2 * TN, tiles // 2 * TN
    units = [("g", 0, 0, a), ("g", 0, a, b), ("d", 0, 0, 0), ("d", 1, 0, 0)]
    at = 0
    for k in range(4):
        w = (tiles + 3 - k) // 4 * TN
        units.append(("g", 1, at, w))
        at += w
    assert at == ff
    count = sum(2 if u[0] == "g" else 1 for u in units)
    big = jax.ShapeDtypeStruct((tokens, ff), BF16)
    wide = jax.ShapeDtypeStruct((tokens, ff), F32)
    h = jax.ShapeDtypeStruct((tokens, d), BF16)
    hT = jax.ShapeDtypeStruct((d, tokens), BF16)
    outs = [jax.ShapeDtypeStruct((2, d, ff), BF16)] * 2 + [jax.ShapeDtypeStruct((2, ff, d), BF16), wide, wide, big, h, hT, hT, big, big, big]

    def kernel(*refs):
        forward_kernel(units, tokens, d, ff, *refs)

    return pl.pallas_call(
        kernel,
        out_shape=outs,
        in_specs=[ANY] * 5,
        out_specs=[ANY] * len(outs),
        scratch_shapes=[
            pltpu.VMEM((tokens, d), BF16), pltpu.VMEM((tokens, d), BF16), pltpu.VMEM((ff, d), BF16),
            pltpu.VMEM(wg.shape, BF16), pltpu.VMEM(wu.shape, BF16), pltpu.VMEM(wd.shape, BF16),
            pltpu.SemaphoreType.DMA((count, 9)), pltpu.SemaphoreType.DMA((count, 9)), pltpu.SemaphoreType.DMA((9,)),
        ],
        compiler_params=pltpu.CompilerParams(collective_id=0, has_side_effects=True, vmem_limit_bytes=60 * 2**20),
        name="forward",
    )(x, dy, wg, wu, wd)


def adamw(w, m, v, g):
    m = 0.9 * m + 0.1 * g
    v = 0.95 * v + 0.05 * g * g
    step = m * lax.rsqrt(v + 1e-8) + 0.1 * w
    return (w - 0.02 * step).astype(BF16), m, v


def scatter(g):
    return lax.psum_scatter(g.astype(BF16), "dp", scatter_dimension=0, tiled=True)


def solution(mesh):
    def step(x, dy, *arrays):
        weights, m, v = (arrays[i : i + 3] for i in (0, 3, 6))
        x, dy = x[0], dy[0]
        WG, WU, WD, gate0, up0, p0, h1, a0T, a1T, p1, dg1, du1 = forward(x, dy, *weights)
        d1 = [scatter(dot(a1T, dg1)), scatter(dot(a1T, du1)), scatter(dot(p1.T, dy))]
        da = lax.dot_general(dg1, WG[1], NT, preferred_element_type=F32).astype(BF16) + lax.dot_general(du1, WU[1], NT, preferred_element_type=F32).astype(BF16)
        wide, da = h1.astype(F32), da.astype(F32)
        scale = lax.rsqrt(jnp.mean(wide * wide, -1, keepdims=True) + 1e-6)
        dh = dy + (scale * (da - wide * (scale * scale * jnp.mean(da * wide, -1, keepdims=True)))).astype(BF16)
        dp = lax.dot_general(dh, WD[0], NT, preferred_element_type=F32).astype(BF16).astype(F32)
        sig = jax.nn.sigmoid(gate0)
        s = gate0 * sig
        du0 = (dp * s).astype(BF16)
        dg0 = (dp * up0 * (sig + s * (1 - sig))).astype(BF16)
        d0 = [scatter(dot(a0T, dg0)), scatter(dot(a0T, du0)), scatter(dot(p0.T, dh))]
        gradients = [jnp.stack([d0[i], d1[i]]).astype(F32) for i in range(3)]
        new = [adamw(w.astype(F32), m, v, g) for w, m, v, g in zip(weights, m, v, gradients, strict=True)]
        return tuple(one[which] for which in range(3) for one in new)

    states, cut = P(("rep", "dp"), None, None), P(None, "dp", None)
    return jax.shard_map(
        step,
        mesh=mesh,
        in_specs=(states, states) + (cut,) * 9,
        out_specs=(P("rep", "dp", None),) * 9,
        check_vma=False,
    )
```

time: 886 us -> 839 us (0.947)
  Pallas kernels: 0 us -> 286 us
  matrix products: 481 us -> 262 us
  waiting for transfers between devices: 329 us -> 244 us
  local copies, waits for them, and re-layouts: 24.5 us -> 2.19 us
    pallas_call x0 -> x1, Pallas kernels: none -> 286 us  [forward(): pl.pallas_call(kernel, out_shape=outs, in_specs=[ANY] * 5, out_specs=[ANY...]
    dot_general x15 -> x9, matrix products: 481 us -> 262 us  [the longest x6 177 us: dot(): return jnp.dot(a, b, preferred_element_type=F32)]
    all_gather x6 -> x0, waiting for transfers between devices: 133 us -> none  [fetched(): lax.all_gather(w[number], 'dp', axis=0, tiled=True)]
    reduce_scatter x6, waiting for transfers between devices: 194 us -> 244 us  [scatter(): lax.psum_scatter(g.astype(BF16), 'dp', scatter_dimension=0, tiled=True)]
    unnamed x26 -> x14, local copies, waits for them, and re-layouts: 16.7 us -> 2.19 us
  transfers between devices with their start and end apart: 12 -> 6, of which waited for: 10 -> 4; matrix products, arithmetic and copies ran while one was open for 43% -> 19% of each run, Pallas kernels for 0% -> 0%
where the time goes in v1:
time: 839 us; the launch traced here: 832 us
  Pallas kernels  286 us (34%)
  matrix products  262 us (31%)
  waiting for transfers between devices  244 us (29%)
  other arithmetic  24.1 us (3%)
  between operations  14.4 us (2%)
    pallas_call x1, Pallas kernels, forward(): pl.pallas_call(kernel, out_shape=outs, in_specs=[ANY] * 5, out_specs=[ANY...  286 us
    reduce_scatter x6, waiting for transfers between devices, scatter(): lax.psum_scatter(g.astype(BF16), 'dp', scatter_dimension=0, tiled=True)  244 us
    dot_general x6, matrix products, dot(): return jnp.dot(a, b, preferred_element_type=F32)  177 us
    dot_general x1, matrix products, step(): lax.dot_general(dh, WD[0], NT, preferred_element_type=F32).astype(BF16)  30.1 us
    dot_general x1, matrix products, step(): lax.dot_general(dg1, WG[1], NT, preferred_element_type=F32).astype(BF16)  28 us
    dot_general x1, matrix products, step(): lax.dot_general(du1, WU[1], NT, preferred_element_type=F32).astype(BF16)  27 us
    convert_element_type x3, other arithmetic, adamw(): return ((w - 0.02 * step).astype(BF16), m, v)  24.1 us
  transfers between devices with their start and end apart: 6, of which 4 were waited for; matrix products, arithmetic and copies ran while one was open for 19% of the time, Pallas kernels for 0%

profile of v1, /device:TPU:0, one launch (start us, length us, event | category | flops | bytes accessed | tf_op | source)
XLA Modules:
  0.0 832.1 jit_solution(3608300249909206834)
XLA Ops:
  7.2 0.0 reduce-scatter.7.cloned.1.call-start
  7.2 285.5 %forward.1 = (bf16[2,896,4864]{2,1,0:T(8,128)(2,1)}, bf16[2,896,4864]{2,1,0:T(8,128)(2,1)}, bf16[2,4864,896]{2,1,0:T(8,128)(2,1)}, f32[2048,4864]{1,0:T(8,128)},...) custom-call(bf16[2048,896]{1,0:T(8,128)(2,1)} %bitcast.37, ...), custom_call_target="tpu_custom_call" | custom-call | tf_op jit(solution)/shard_map/forward/pallas_call | solution.py:254
  292.8 0.0 copy-start.6
  292.8 27.0 %fusion.15 = bf16[2048,896]{1,0:T(8,128)(2,1)S(1)} fusion(bf16[2048,4864]{1,0:T(8,128)(2,1)} %get-tuple-element.25, bf16[2,896,4864]{2,1,0:T(8,128)(2,1)} %get-tuple-element.26), kind=kOutput, calls=%fused_computation.21 | convolution fusion | flops 17850957824 | bytes 32309248 | tf_op jit(solution)/shard_map/dot_general | solution.py:286
  319.8 0.0 copy-done.6
  319.8 28.0 %fusion.24 = (f32[2048]{0:T(1024)S(1)}, f32[2048]{0:T(1024)S(1)}, bf16[2048,896]{1,0:T(8,128)(2,1)}) fusion(bf16[2048,896]{1,0:T(8,128)(2,1)S(1)} %copy-done.6, bf16[2048,896]{1,0:T(8,128)(2,1)S(1)} %fusion.15, bf16[2048,4864]{1,0:T(8,128)(2,1)} %get-tuple-element.23, bf16[2,896,4864]{2,1,0:T(8,128)(2,1)} %get-tuple-element.24), kind=kOutput, calls=%fused_computation.30 | convolution fusion | flops 17865633792 | bytes 39665664 | tf_op jit(solution)/shard_map/dot_general | solution.py:286
  347.8 0.0 copy-start.2
  347.8 0.0 copy-start.4
  347.8 30.1 %convolution_convert_fusion = bf16[2048,4864]{1,0:T(8,128)(2,1)} fusion(bf16[2,4864,896]{2,1,0:T(8,128)(2,1)} %get-tuple-element.27, bf16[2048,896]{1,0:T(8,128)(2,1)} %get-tuple-element.22, bf16[2048,896]{1,0:T(8,128)(2,1)} %get-tuple-element.46, f32[2048]{0:T(1024)S(1)} %get-tuple-element.45, f32[2048]{0:T(1024)S(1)} %get-tuple-element.44, ...), kind=kOutput, calls=%fused_computation.9 | convolution fusion | flops 17873764352 | bytes 39665664 | tf_op jit(solution)/shard_map/dot_general | solution.py:290
  378.0 0.0 copy-done.2
  378.0 0.0 copy-done.4
  378.0 38.2 %fusion.8 = bf16[896,4864]{1,0:T(8,128)(2,1)} fusion(bf16[896,2048]{1,0:T(8,128)(2,1)} %get-tuple-element.21, f32[2048,4864]{1,0:T(8,128)} %get-tuple-element.28, bf16[2048,4864]{1,0:T(8,128)(2,1)} %convolution_convert_fusion, f32[2048,4864]{1,0:T(8,128)} %get-tuple-element.29), kind=kOutput, calls=%fused_computation.14 | convolution fusion | flops 17964892160 | bytes 112001024 | tf_op jit(solution)/shard_map/dot_general | solution.py:16
  416.2 0.0 reduce-scatter.7.cloned.1.call-update
  416.2 0.0 reduce-scatter.9.cloned.1.call-start
  416.3 24.8 %convolution_convert_fusion.4 = bf16[896,4864]{1,0:T(8,128)(2,1)} fusion(bf16[896,2048]{1,0:T(8,128)(2,1)} %get-tuple-element.30, bf16[2048,4864]{1,0:T(8,128)(2,1)} %get-tuple-element.23), kind=kOutput, calls=%fused_computation.19 | convolution fusion | flops 17855315968 | bytes 32309248 | tf_op jit(solution)/shard_map/dot_general | solution.py:16
  441.1 0.0 reduce-scatter.9.cloned.1.call-update
  441.1 0.0 reduce-scatter.11.cloned.1.call-start
  441.2 30.2 %fusion.11 = bf16[896,4864]{1,0:T(8,128)(2,1)} fusion(bf16[896,2048]{1,0:T(8,128)(2,1)} %get-tuple-element.21, bf16[2048,4864]{1,0:T(8,128)(2,1)} %convolution_convert_fusion, f32[2048,4864]{1,0:T(8,128)} %get-tuple-element.29), kind=kOutput, calls=%fused_computation.15 | convolution fusion | flops 17925046272 | bytes 72155136 | tf_op jit(solution)/shard_map/dot_general | solution.py:16
  471.4 0.0 reduce-scatter.11.cloned.1.call-update
  471.4 0.0 reduce-scatter.13.cloned.1.call-start
  471.5 25.0 %convolution_convert_fusion.3 = bf16[896,4864]{1,0:T(8,128)(2,1)} fusion(bf16[896,2048]{1,0:T(8,128)(2,1)} %get-tuple-element.30, bf16[2048,4864]{1,0:T(8,128)(2,1)} %get-tuple-element.25), kind=kOutput, calls=%fused_computation.18 | convolution fusion | flops 17855315968 | bytes 32309248 | tf_op jit(solution)/shard_map/dot_general | solution.py:16
  496.5 0.0 reduce-scatter.13.cloned.1.call-update
  496.5 0.0 reduce-scatter.17.cloned.1.call-start
  496.6 27.5 %convolution_convert_fusion.1 = bf16[4864,896]{1,0:T(8,128)(2,1)} fusion(bf16[2048,4864]{1,0:T(8,128)(2,1)} %get-tuple-element.32, bf16[1,2048,896]{2,1,0:T(8,128)(2,1)} %param.12), kind=kOutput, calls=%fused_computation.16 | convolution fusion | flops 17855315968 | bytes 32309248 | tf_op jit(solution)/shard_map/dot_general | solution.py:16
  524.0 0.0 copy-start.3
  524.0 0.0 copy-start.5
  524.0 0.0 reduce-scatter.17.cloned.1.call-update
  524.0 0.0 reduce-scatter.15.cloned.1.call-start
  524.1 0.6 copy-done.3
  524.7 0.0 copy-done.5
  524.7 30.8 %convolution_convert_fusion.2 = bf16[4864,896]{1,0:T(8,128)(2,1)} fusion(bf16[2048,4864]{1,0:T(8,128)(2,1)} %get-tuple-element.31, bf16[2048,896]{1,0:T(8,128)(2,1)} %get-tuple-element.22, bf16[2048,896]{1,0:T(8,128)(2,1)} %get-tuple-element.46, f32[2048]{0:T(1024)S(1)} %copy-done.5, f32[2048]{0:T(1024)S(1)} %copy-done.3, bf16[1,2048,896]{2,1,0:T(8,128)(2,1)} %param.12), kind=kOutput, calls=%fused_computation.17 | convolution fusion | flops 17868161024 | bytes 39665664 | tf_op jit(solution)/shard_map/dot_general | solution.py:16
  555.5 0.0 copy-start
  555.5 0.0 reduce-scatter.15.cloned.1.call-update
  555.5 0.0 reduce-scatter.7.cloned.1.call-done
  555.6 0.0 reduce-scatter.9.cloned.1.call-done
  555.6 1.5 copy-done
  557.1 7.8 fusion.28
  565.0 50.3 %reduce-scatter.11.cloned.1.call-done = bf16[112,4864]{1,0:T(8,128)(2,1)} async-done(((bf16[896,4864]{1,0:T(8,128)(2,1)}), bf16[112,4864]{1,0:T(8,128)(2,1)}) %reduce-scatter.11.cloned.1.call-update) | async-done | bytes 1089552 | tf_op jit(solution)/shard_map/reduce_scatter | solution.py:277
  615.3 67.3 %reduce-scatter.13.cloned.1.call-done = bf16[112,4864]{1,0:T(8,128)(2,1)} async-done(((bf16[896,4864]{1,0:T(8,128)(2,1)}), bf16[112,4864]{1,0:T(8,128)(2,1)}) %reduce-scatter.13.cloned.1.call-update) | async-done | bytes 1089552 | tf_op jit(solution)/shard_map/reduce_scatter | solution.py:277
  682.6 0.0 copy-start.1
  682.6 8.4 %fusion.32 = (bf16[2,112,4864]{2,1,0:T(8,128)(2,1)}, f32[2,112,4864]{2,1,0:T(8,128)}, f32[2,112,4864]{2,1,0:T(8,128)}) fusion(bf16[2,112,4864]{2,1,0:T(8,128)(2,1)} %refs_3_.1, bf16[1,112,4864]{2,1,0:T(8,128)(2,1)} %bitcast.43, bf16[1,112,4864]{2,1,0:T(8,128)(2,1)} %bitcast.41, f32[2,112,4864]{2,1,0:T(8,128)} %param.20, f32[2,112,4864]{2,1,0:T(8,128)} %param.17), kind=kLoop, calls=%fused_computation.50 | loop fusion | flops 20701184 | bytes 23969792 | tf_op jit(solution)/shard_map/convert_element_type | solution.py:273
  691.0 58.9 %reduce-scatter.17.cloned.1.call-done = bf16[608,896]{1,0:T(8,128)(2,1)} async-done(((bf16[4864,896]{1,0:T(8,128)(2,1)}), bf16[608,896]{1,0:T(8,128)(2,1)}) %reduce-scatter.17.cloned.1.call-update) | async-done | bytes 1089552 | tf_op jit(solution)/shard_map/reduce_scatter | solution.py:277
  749.9 67.3 %reduce-scatter.15.cloned.1.call-done = bf16[608,896]{1,0:T(8,128)(2,1)} async-done(((bf16[4864,896]{1,0:T(8,128)(2,1)}), bf16[608,896]{1,0:T(8,128)(2,1)}) %reduce-scatter.15.cloned.1.call-update) | async-done | bytes 1089552 | tf_op jit(solution)/shard_map/reduce_scatter | solution.py:277
  817.2 0.0 copy-done.1
  817.2 7.9 fusion.36
  (1 shorter events, 0.0 us)
Async XLA Ops:
  7.2 548.4 %reduce-scatter.7.cloned.1.call-start = ((), (), s32[]{:S(2)}) async-start(), calls=%async_computation.6 | async-start | bytes 9805824 | tf_op jit(solution)/shard_map/reduce_scatter | solution.py:277
  292.8 27.0 %copy-start.6 = (bf16[2048,896]{1,0:T(8,128)(2,1)S(1)}, bf16[2048,896]{1,0:T(8,128)(2,1)}, u32[]{:S(2)}) copy-start(bf16[2048,896]{1,0:T(8,128)(2,1)} %get-tuple-element.22) | copy-start | bytes 11010052
  347.8 30.2 %copy-start.2 = (f32[2048]{0:T(1024)}, f32[2048]{0:T(1024)S(1)}, u32[]{:S(2)}) copy-start(f32[2048]{0:T(1024)S(1)} %get-tuple-element.44) | copy-start | bytes 24580
  347.8 30.2 %copy-start.4 = (f32[2048]{0:T(1024)}, f32[2048]{0:T(1024)S(1)}, u32[]{:S(2)}) copy-start(f32[2048]{0:T(1024)S(1)} %get-tuple-element.45) | copy-start | bytes 24580
  416.2 139.4 %reduce-scatter.9.cloned.1.call-start = ((), (), s32[]{:S(2)}) async-start(), calls=%async_computation.7 | async-start | bytes 9805824 | tf_op jit(solution)/shard_map/reduce_scatter | solution.py:277
  441.1 174.1 %reduce-scatter.11.cloned.1.call-start = ((), (), s32[]{:S(2)}) async-start(), calls=%async_computation.8 | async-start | bytes 9805824 | tf_op jit(solution)/shard_map/reduce_scatter | solution.py:277
  471.4 211.2 %reduce-scatter.13.cloned.1.call-start = ((), (), s32[]{:S(2)}) async-start(), calls=%async_computation.9 | async-start | bytes 9805824 | tf_op jit(solution)/shard_map/reduce_scatter | solution.py:277
  496.5 253.4 %reduce-scatter.17.cloned.1.call-start = ((), (), s32[]{:S(2)}) async-start(), calls=%async_computation.11 | async-start | bytes 9805824 | tf_op jit(solution)/shard_map/reduce_scatter | solution.py:277
  524.0 0.7 copy-start.3
  524.0 0.7 copy-start.5
  524.0 293.2 %reduce-scatter.15.cloned.1.call-start = ((), (), s32[]{:S(2)}) async-start(), calls=%async_computation.10 | async-start | bytes 9805824 | tf_op jit(solution)/shard_map/reduce_scatter | solution.py:277
  555.5 1.6 copy-start
  682.6 134.6 %copy-start.1 = (bf16[2,608,896]{2,1,0:T(8,128)(2,1)S(1)}, bf16[2,608,896]{2,1,0:T(8,128)(2,1)}, u32[]{:S(2)}) copy-start(bf16[2,608,896]{2,1,0:T(8,128)(2,1)} %refs_4_.1) | copy-start | bytes 6537220
Sparse Core Ops, SparseCore 0:
  416.3 63.9 reduce-scatter.6
  483.9 63.9 reduce-scatter.8
  551.3 63.9 reduce-scatter.10
  618.6 63.9 reduce-scatter.12
  685.9 63.9 reduce-scatter.16
  753.2 63.9 reduce-scatter.14

commit v2 on v1

--- a/solution.py
+++ b/solution.py
@@ -266,6 +266,296 @@
     )(x, dy, wg, wu, wd)
 
 
+class Unit:
+    def __init__(self, n, slot, bufs, rows, width, by_rows, outs, older, newer):
+        self.n, self.slot, self.rows, self.width, self.by_rows, self.outs, self.older, self.newer = n, slot, rows, width, by_rows, outs, older, newer
+        self.G, self.Rp, self.R1, self.R2 = bufs
+        self.pieces = len(outs)
+        self.h = (rows if by_rows else width) // 2
+
+    def block(self, b):
+        return self.G.at[:, pl.ds(pl.multiple_of(b * self.rows, 16), self.rows), pl.ds(0, self.width)]
+
+    def half(self, b, part):
+        if self.by_rows:
+            return self.G.at[:, pl.ds(pl.multiple_of(b * self.rows + part * self.h, 16), self.h), :]
+        return self.G.at[:, pl.ds(pl.multiple_of(b * self.rows, 16), self.rows), pl.ds(part * self.h, self.h)]
+
+    def narrow(self, ref):
+        return ref if self.by_rows else ref.at[:, :, pl.ds(0, self.h)]
+
+    def r1(self, part, which):
+        return self.narrow(self.R1.at[part, which])
+
+    def r2(self, part):
+        return self.narrow(self.R2.at[part])
+
+    def rp(self, q):
+        return self.Rp.at[q, :, :, pl.ds(0, self.width)]
+
+
+def backward_kernel(groups, tokens, d, ff, p1, dg1, du1, a1T, dy, WG, WU, WD, h1, gate0, up0, p0, a0T, gG, gU, gD,
+                    aT_vm, dh_vm, Gg, Rpg, R1g, R2g, Gd, Rpd, R1d, R2d, send, recv, local, credit):
+    me, flip = around()
+    xn, yn, pn = flip(me, 4), flip(me, 2), flip(me, 1)
+    core, q0 = me % 2, me // 2
+    qx, qy = flip(q0, 2), flip(q0, 1)
+    qd = flip(qx, 1)
+    rg, rd = d // 8, ff // 8
+    SLOTS = Gg.shape[0]
+
+    barrier = pltpu.get_barrier_semaphore()
+    for other in (xn, yn, pn):
+        pl.semaphore_signal(barrier, inc=1, device_id={"dp": other}, device_id_type=pl.DeviceIdType.MESH)
+    pl.semaphore_wait(barrier, 3)
+
+    down_bufs = (Gd, Rpd, R1d, R2d)
+    count = len(groups)
+    D = [Unit(2 * count + 1, SLOTS, down_bufs, rd, d, True, [gD.at[0]], True, False),
+         Unit(2 * count, SLOTS, down_bufs, rd, d, True, [gD.at[1]], False, True)]
+    units = []
+    for layer in (1, 0):
+        for at, width in groups:
+            n = len(units)
+            s = n % SLOTS
+            cols = pl.ds(at, width)
+            units.append(Unit(n, s, (Gg.at[s], Rpg.at[s], R1g.at[s], R2g.at[s]), rg, width, False,
+                              [gG.at[layer, :, cols], gU.at[layer, :, cols]], n >= SLOTS, n + SLOTS < 2 * count))
+
+    def remote(u, k, src, dst, to):
+        return pltpu.make_async_remote_copy(src_ref=src, dst_ref=dst, send_sem=send.at[u.n, k], recv_sem=recv.at[u.n, k],
+                                            device_id={"dp": to}, device_id_type=pl.DeviceIdType.MESH)
+
+    def to_partner(u, q):
+        return remote(u, q, u.block(2 * q + 1 - core), u.rp(q), pn)
+
+    def stage1(u, k):
+        q, part, which, to = ((qd, 0, 1, xn), (qd, 1, 1, yn), (qx, 0, 0, xn), (qy, 1, 0, yn))[k]
+        return remote(u, 4 + k, u.half(2 * q + core, part), u.r1(part, which), to)
+
+    def stage2(u, k):
+        q, to = ((qy, yn), (qx, xn))[k]
+        return remote(u, 8 + k, u.half(2 * q + core, k), u.r2(k), to)
+
+    def grant(u, k, to):
+        pl.semaphore_signal(credit.at[u.slot, k], inc=1, device_id={"dp": to}, device_id_type=pl.DeviceIdType.MESH)
+
+    def add(dst, *others):
+        for i in range(dst.shape[0]):
+            total = dst[i].astype(F32)
+            for other in others:
+                total = total + other[i].astype(F32)
+            dst[i] = total.astype(BF16)
+
+    def s0(u):
+        if u.older:
+            pl.semaphore_wait(credit.at[u.slot, 0], 1)
+        for q in range(4):
+            to_partner(u, q).start()
+
+    def s1(u):
+        for q in range(4):
+            to_partner(u, q).wait_recv()
+
+        @pl.loop(0, 4)
+        def _(q):
+            add(u.block(2 * q + core), u.rp(q))
+        if u.newer:
+            grant(u, 0, pn)
+        if u.older:
+            pl.semaphore_wait(credit.at[u.slot, 1], 1)
+            pl.semaphore_wait(credit.at[u.slot, 2], 1)
+        for k in range(4):
+            stage1(u, k).start()
+
+    def s2(u):
+        stage1(u, 0).wait_recv()
+        add(u.half(2 * qy + core, 0), u.r1(0, 1))
+        stage2(u, 0).start()
+        stage1(u, 1).wait_recv()
+        add(u.half(2 * qx + core, 1), u.r1(1, 1))
+        stage2(u, 1).start()
+
+    def out(u, i):
+        return pltpu.make_async_copy(u.block(me).at[i], u.outs[i], local.at[u.n, i])
+
+    def s3(u):
+        for k in (2, 3):
+            stage1(u, k).wait_recv()
+        for part in (0, 1):
+            stage2(u, part).wait_recv()
+            add(u.half(me, part), u.r1(part, 0), u.r2(part))
+        for i in range(u.pieces):
+            out(u, i).start()
+        if u.newer:
+            grant(u, 1, xn)
+            grant(u, 2, yn)
+        for q in range(4):
+            to_partner(u, q).wait_send()
+        for k in range(4):
+            stage1(u, k).wait_send()
+        for k in range(2):
+            stage2(u, k).wait_send()
+
+    def s4(u):
+        for i in range(u.pieces):
+            out(u, i).wait()
+
+    def run(events, j):
+        for at in sorted({e[0] for e in events}):
+            @pl.when(j == at)
+            def _(at=at):
+                for when, what, u in events:
+                    if when == at:
+                        what(u)
+
+    TM = 512
+    wide_tile = pl.BlockSpec((tokens, TN), lambda j: (0, j))
+    w_tile = pl.BlockSpec((d, TN), lambda j: (0, j))
+
+    def load(src, dst):
+        c = pltpu.make_async_copy(src, dst, local.at[0, 0])
+        c.start()
+        c.wait()
+
+    def down_weight(p, unit, events):
+        def body(idx, p_t):
+            j = idx.index[0]
+            run(events, j)
+            g = lax.dot_general(p_t[...], dh_vm[...], (((0,), (0,)), ((), ())), preferred_element_type=F32)
+            unit.G[0, pl.ds(pl.multiple_of(j * TN, TN), TN), :] = g.astype(BF16)
+        pltpu.emit_pipeline(body, grid=(ff // TN,), in_specs=[wide_tile], _explicit_indices=True)(p)
+
+    def store_weight(mine, j, i, g_t):
+        value = dot(aT_vm[...], g_t[...]).astype(BF16)
+        for k, u in enumerate(mine):
+            at, width = groups[k]
+
+            @pl.when((j >= at // TN) & (j < (at + width) // TN))
+            def _(u=u, at=at):
+                u.G[i, :, pl.ds(pl.multiple_of(j * TN - at, TN), TN)] = value
+
+    def layer1(acc, events):
+        mine = units[:count]
+
+        def body(idx, dg_t, du_t, wg_t, wu_t):
+            j = idx.index[0]
+            run(events, j)
+            store_weight(mine, j, 0, dg_t)
+            store_weight(mine, j, 1, du_t)
+
+            def both(i):
+                rows = pl.ds(pl.multiple_of(i * TM, TM), TM)
+                return rows, lax.dot_general(dg_t[rows, :], wg_t[...], NT, preferred_element_type=F32) + lax.dot_general(
+                    du_t[rows, :], wu_t[...], NT, preferred_element_type=F32)
+
+            @pl.loop(0, tokens // TM)
+            def _(i):
+                rows, value = both(i)
+                acc[rows, :] = jnp.where(j == 0, value, acc[rows, :] + value)
+        pltpu.emit_pipeline(body, grid=(ff // TN,), in_specs=[wide_tile, wide_tile, w_tile, w_tile], _explicit_indices=True)(dg1, du1, WG.at[1], WU.at[1])
+
+        def norm(idx, h_t):
+            rows = pl.ds(pl.multiple_of(idx.index[0] * TN, TN), TN)
+            wide = h_t[...].astype(F32)
+            da = acc[rows, :].astype(BF16).astype(F32)
+            scale = lax.rsqrt(jnp.mean(wide * wide, -1, keepdims=True) + 1e-6)
+            back = scale * (da - wide * (scale * scale * jnp.mean(da * wide, -1, keepdims=True)))
+            dh_vm[rows, :] = dh_vm[rows, :] + back.astype(BF16)
+        pltpu.emit_pipeline(norm, grid=(tokens // TN,), in_specs=[pl.BlockSpec((TN, d), lambda i: (i, 0))], _explicit_indices=True)(h1)
+
+    def layer0(dg_vm, du_vm, events):
+        mine = units[count:]
+
+        def body(idx, wd_t, gate_t, up_t):
+            j = idx.index[0]
+            run(events, j)
+
+            @pl.loop(0, tokens // TM)
+            def _(i):
+                rows = pl.ds(pl.multiple_of(i * TM, TM), TM)
+                dp = lax.dot_general(dh_vm[rows, :], wd_t[...], NT, preferred_element_type=F32).astype(BF16).astype(F32)
+                g = gate_t[rows, :]
+                sig = jax.nn.sigmoid(g)
+                s = g * sig
+                du_vm[rows, :] = (dp * s).astype(BF16)
+                dg_vm[rows, :] = (dp * up_t[rows, :] * (sig + s * (1 - sig))).astype(BF16)
+            store_weight(mine, j, 0, dg_vm)
+            store_weight(mine, j, 1, du_vm)
+        pltpu.emit_pipeline(body, grid=(ff // TN,), in_specs=[pl.BlockSpec((TN, d), lambda j: (j, 0)), wide_tile, wide_tile], _explicit_indices=True)(
+            WD.at[0], gate0, up0)
+
+    tiles = ff // TN
+    order = {"D1": [], "L1": [], "D0": [], "L0": [], "end": []}
+
+    def spot(tick):
+        if tick < tiles:
+            return "L1", tick
+        tick -= tiles
+        if tick < 5:
+            return "D0", 4 * tick
+        tick -= 5
+        return ("L0", tick) if tick < tiles else ("end", tick)
+
+    def plan(u, ticks):
+        for tick, what in zip(ticks, (s0, s1, s2, s3, s4)):
+            where, at = spot(tick)
+            order[where].append((at, what, u))
+
+    plan(D[1], (0, 2, 9, 12, 14))
+    for k, u in enumerate(units):
+        at, width = groups[k % count]
+        end = (at + width) // TN + (0 if k < count else tiles + 5)
+        plan(u, (end, end + 1, end + 5, end + 7, end + 8))
+    start = tiles + 5
+    plan(D[0], (start, start + 2, start + 9, start + 12, start + 14))
+    for events in order.values():
+        events.sort(key=lambda e: (e[0], -(s0, s1, s2, s3, s4).index(e[1])))
+
+    load(dy, dh_vm)
+    load(a1T, aT_vm)
+    down_weight(p1, D[1], [])
+    pl.run_scoped(lambda acc: layer1(acc, order["L1"]), pltpu.VMEM((tokens, d), F32))
+    load(a0T, aT_vm)
+    down_weight(p0, D[0], order["D0"])
+    pl.run_scoped(lambda a, b: layer0(a, b, order["L0"]), pltpu.VMEM((tokens, TN), BF16), pltpu.VMEM((tokens, TN), BF16))
+    for _, what, u in order["end"]:
+        what(u)
+
+
+def backward(p1, dg1, du1, a1T, dy, WG, WU, WD, h1, gate0, up0, p0, a0T):
+    tokens, d = dy.shape
+    ff = dg1.shape[1]
+    tiles, groups, at = ff // TN, [], 0
+    while at < ff:
+        width = min(4 * TN, ff - at)
+        groups.append((at, width))
+        at += width
+    C, rg, rd, slots, n = 4 * TN, d // 8, ff // 8, 3, 2 * len(groups) + 2
+    outs = [jax.ShapeDtypeStruct((2, rg, ff), BF16)] * 2 + [jax.ShapeDtypeStruct((2, rd, d), BF16)]
+
+    def kernel(*refs):
+        backward_kernel(groups, tokens, d, ff, *refs)
+
+    return pl.pallas_call(
+        kernel,
+        out_shape=outs,
+        in_specs=[ANY] * 13,
+        out_specs=[ANY] * 3,
+        scratch_shapes=[
+            pltpu.VMEM((d, tokens), BF16), pltpu.VMEM((tokens, d), BF16),
+            pltpu.VMEM((slots, 2, d, C), BF16), pltpu.VMEM((slots, 4, 2, rg, C), BF16),
+            pltpu.VMEM((slots, 2, 2, 2, rg, C // 2), BF16), pltpu.VMEM((slots, 2, 2, rg, C // 2), BF16),
+            pltpu.VMEM((1, ff, d), BF16), pltpu.VMEM((4, 1, rd, d), BF16),
+            pltpu.VMEM((2, 2, 1, rd // 2, d), BF16), pltpu.VMEM((2, 1, rd // 2, d), BF16),
+            pltpu.SemaphoreType.DMA((n, 10)), pltpu.SemaphoreType.DMA((n, 10)), pltpu.SemaphoreType.DMA((n, 2)),
+            pltpu.SemaphoreType.REGULAR((slots + 1, 3)),
+        ],
+        compiler_params=pltpu.CompilerParams(collective_id=1, has_side_effects=True, vmem_limit_bytes=67000000),
+        name="backward",
+    )(p1, dg1, du1, a1T, dy, WG, WU, WD, h1, gate0, up0, p0, a0T)
+
+
 def adamw(w, m, v, g):
     m = 0.9 * m + 0.1 * g
     v = 0.95 * v + 0.05 * g * g
@@ -273,27 +563,12 @@
     return (w - 0.02 * step).astype(BF16), m, v
 
 
-def scatter(g):
-    return lax.psum_scatter(g.astype(BF16), "dp", scatter_dimension=0, tiled=True)
-
-
 def solution(mesh):
     def step(x, dy, *arrays):
         weights, m, v = (arrays[i : i + 3] for i in (0, 3, 6))
         x, dy = x[0], dy[0]
         WG, WU, WD, gate0, up0, p0, h1, a0T, a1T, p1, dg1, du1 = forward(x, dy, *weights)
-        d1 = [scatter(dot(a1T, dg1)), scatter(dot(a1T, du1)), scatter(dot(p1.T, dy))]
-        da = lax.dot_general(dg1, WG[1], NT, preferred_element_type=F32).astype(BF16) + lax.dot_general(du1, WU[1], NT, preferred_element_type=F32).astype(BF16)
-        wide, da = h1.astype(F32), da.astype(F32)
-        scale = lax.rsqrt(jnp.mean(wide * wide, -1, keepdims=True) + 1e-6)
-        dh = dy + (scale * (da - wide * (scale * scale * jnp.mean(da * wide, -1, keepdims=True)))).astype(BF16)
-        dp = lax.dot_general(dh, WD[0], NT, preferred_element_type=F32).astype(BF16).astype(F32)
-        sig = jax.nn.sigmoid(gate0)
-        s = gate0 * sig
-        du0 = (dp * s).astype(BF16)
-        dg0 = (dp * up0 * (sig + s * (1 - sig))).astype(BF16)
-        d0 = [scatter(dot(a0T, dg0)), scatter(dot(a0T, du0)), scatter(dot(p0.T, dh))]
-        gradients = [jnp.stack([d0[i], d1[i]]).astype(F32) for i in range(3)]
+        gradients = [g.astype(F32) for g in backward(p1, dg1, du1, a1T, dy, WG, WU, WD, h1, gate0, up0, p0, a0T)]
         new = [adamw(w.astype(F32), m, v, g) for w, m, v, g in zip(weights, m, v, gradients, strict=True)]
         return tuple(one[which] for which in range(3) for one in new)
 

time: 839 us -> 685 us (0.82)
  Pallas kernels: 286 us -> 657 us
  matrix products: 262 us -> 0 us
  waiting for transfers between devices: 244 us -> 0 us
  between operations: 14.4 us -> 0.68 us
    pallas_call x0 -> x1, Pallas kernels: none -> 372 us  [backward(): pl.pallas_call(kernel, out_shape=outs, in_specs=[ANY] * 13, out_specs=[AN...]
    dot_general x9 -> x0, matrix products: 262 us -> none  [the longest x6 177 us: dot(): return jnp.dot(a, b, preferred_element_type=F32)]
    reduce_scatter x6 -> x0, waiting for transfers between devices: 244 us -> none  [scatter(): lax.psum_scatter(g.astype(BF16), 'dp', scatter_dimension=0, tiled=True)]
    convert_element_type x3 -> x2, other arithmetic: 24.1 us -> 24.3 us  [adamw(): return ((w - 0.02 * step).astype(BF16), m, v)]
  transfers between devices with their start and end apart: 6 -> 0, of which waited for: 4 -> 0; matrix products, arithmetic and copies ran while one was open for 19% -> 0% of each run, Pallas kernels for 0% -> 0%
where the time goes in v2:
time: 685 us; the launch traced here: 684 us
  Pallas kernels  657 us (96%)
  other arithmetic  24.3 us (4%)
    pallas_call x1, Pallas kernels, backward(): pl.pallas_call(kernel, out_shape=outs, in_specs=[ANY] * 13, out_specs=[AN...  372 us
    pallas_call x1, Pallas kernels, forward(): pl.pallas_call(kernel, out_shape=outs, in_specs=[ANY] * 5, out_specs=[ANY...  285 us
    convert_element_type x2, other arithmetic, adamw(): return ((w - 0.02 * step).astype(BF16), m, v)  24.3 us

profile of v2, /device:TPU:0, one launch (start us, length us, event | category | flops | bytes accessed | tf_op | source)
XLA Modules:
  0.0 683.7 jit_solution(9324114503695874856)
XLA Ops:
  0.6 285.5 %forward.1 = (bf16[2,896,4864]{2,1,0:T(8,128)(2,1)}, bf16[2,896,4864]{2,1,0:T(8,128)(2,1)}, bf16[2,4864,896]{2,1,0:T(8,128)(2,1)}, f32[2048,4864]{1,0:T(8,128)},...) custom-call(bf16[2048,896]{1,0:T(8,128)(2,1)} %bitcast.4, ...), custom_call_target="tpu_custom_call" | custom-call | tf_op jit(solution)/shard_map/forward/pallas_call | solution.py:254
  286.1 371.9 %backward.1 = (bf16[2,112,4864]{2,1,0:T(8,128)(2,1)}, bf16[2,112,4864]{2,1,0:T(8,128)(2,1)}, bf16[2,608,896]{2,1,0:T(8,128)(2,1)}) custom-call(bf16[2048,4864]{1,0:T(8,128)(2,1)} %get-tuple-element.24.refs_0_, bf16[2048,4864]{1,0:T(8,128)(2,1)} %get-tuple-element.25.refs_1_, bf16[2048,4864]{1,0:T(8,128)(2,1)} %get-tuple-element.26.refs_2_, ...), custom_call_target="tpu_custom_call" | custom-call | tf_op jit(solution)/shard_map/backward/pallas_call | solution.py:540
  658.0 0.0 copy-start
  658.0 0.0 copy-start.1
  658.0 0.0 copy-start.2
  658.0 9.2 %fusion.10 = (bf16[2,608,896]{2,1,0:T(8,128)(2,1)}, f32[2,608,896]{2,1,0:T(8,128)}, f32[2,608,896]{2,1,0:T(8,128)}) fusion(bf16[2,608,896]{2,1,0:T(8,128)(2,1)} %refs_4_.1, bf16[2,608,896]{2,1,0:T(8,128)(2,1)} %get-tuple-element.38, f32[2,608,896]{2,1,0:T(8,128)} %param.21, f32[2,608,896]{2,1,0:T(8,128)} %param.18), kind=kLoop, calls=%fused_computation.22 | loop fusion | flops 17432576 | bytes 23969792 | tf_op jit(solution)/shard_map/convert_element_type | solution.py:563
  667.2 0.0 copy-done
  667.2 0.2 copy-done.1
  667.4 1.2 copy-done.2
  668.6 15.1 %fusion.2 = (bf16[2,112,4864]{2,1,0:T(8,128)(2,1)}, f32[2,112,4864]{2,1,0:T(8,128)}, f32[2,112,4864]{2,1,0:T(8,128)}, bf16[2,112,4864]{2,1,0:T(8,128)(2,1)}, f32...) fusion(bf16[2,112,4864]{2,1,0:T(8,128)(2,1)S(1)} %copy-done, bf16[2,112,4864]{2,1,0:T(8,128)(2,1)S(1)} %copy-done.2, ...), kind=kLoop, calls=%fused_computation.14 | loop fusion | flops 34865152 | bytes 47939584 | tf_op jit(solution)/shard_map/convert_element_type | solution.py:563
Async XLA Ops:
  658.0 9.2 %copy-start = (bf16[2,112,4864]{2,1,0:T(8,128)(2,1)S(1)}, bf16[2,112,4864]{2,1,0:T(8,128)(2,1)}, u32[]{:S(2)}) copy-start(bf16[2,112,4864]{2,1,0:T(8,128)(2,1)} %refs_2_.1) | copy-start | bytes 6537220
  658.0 9.4 %copy-start.1 = (bf16[2,112,4864]{2,1,0:T(8,128)(2,1)S(1)}, bf16[2,112,4864]{2,1,0:T(8,128)(2,1)}, u32[]{:S(2)}) copy-start(bf16[2,112,4864]{2,1,0:T(8,128)(2,1)} %refs_3_.1) | copy-start | bytes 6537220
  658.0 10.6 %copy-start.2 = (bf16[2,112,4864]{2,1,0:T(8,128)(2,1)S(1)}, bf16[2,112,4864]{2,1,0:T(8,128)(2,1)}, u32[]{:S(2)}) copy-start(bf16[2,112,4864]{2,1,0:T(8,128)(2,1)} %get-tuple-element.36) | copy-start | bytes 6537220

commit v3 on v2

--- a/solution.py
+++ b/solution.py
@@ -8,8 +8,9 @@
 NAMES = ("w_gate", "w_up", "w_down")
 F32, BF16 = jnp.float32, jnp.bfloat16
 TN = 256
+GROUP = 3 * TN
 ANY = pl.BlockSpec(memory_space=pl.ANY)
-NT = (((1,), (1,)), ((), ()))
+NT, TT = (((1,), (1,)), ((), ())), (((0,), (0,)), ((), ()))
 
 
 def dot(a, b):
@@ -51,8 +52,8 @@
         return self.full.at[self.layer, pl.ds(pl.multiple_of(owner * self.rows + off, 16), n), cols]
 
 
-def forward_kernel(units, tokens, d, ff, x, dy, wg, wu, wd, WG, WU, WD, gate0, up0, p0, h1, a0T, a1T, p1, dg1, du1,
-                   a_vm, dy_vm, wd_vm, own_g, own_u, own_d, send, recv, local):
+def forward_kernel(units, tokens, d, ff, x, dy, wg, wu, wd, WG, WU, WD, f0, e0, p0, h1, a0T, a1T, gd1, dg1, du1,
+                   a_vm, dy_vm, wd_vm, p_vm, own_g, own_u, own_d, send, recv, local):
     me, flip = around()
     xn, yn, pn = flip(me, 4), flip(me, 2), flip(me, 1)
     diag = flip(xn, 2)
@@ -156,23 +157,25 @@
             transpose_out(idx.index[0], out)
         pltpu.emit_pipeline(body, grid=(tokens // TN,), out_specs=[pl.BlockSpec((d, TN), lambda j: (0, j))], _explicit_indices=True)(aT)
 
-    TM = 512
+    TM, TMD = 1024, 512
 
     def gate_up(at, width):
-        def body(wg_t, wu_t, gate_t, up_t, p_t):
+        def body(wg_t, wu_t, f_t, e_t, p_t):
             @pl.loop(0, tokens // TM)
             def _(i):
                 rows = pl.ds(pl.multiple_of(i * TM, TM), TM)
                 a = a_vm[rows, :]
                 g = dot(a, wg_t[...])
                 u = dot(a, wu_t[...])
-                gate_t[rows, :] = g
-                up_t[rows, :] = u
-                p_t[rows, :] = (g * jax.nn.sigmoid(g) * u).astype(BF16)
+                sig = jax.nn.sigmoid(g)
+                s = g * sig
+                f_t[rows, :] = s
+                e_t[rows, :] = u * (sig + s * (1 - sig))
+                p_t[rows, :] = (s * u).astype(BF16)
         j0 = at // TN
         w = pl.BlockSpec((d, TN), lambda j: (0, j + j0))
         o = pl.BlockSpec((tokens, TN), lambda j: (0, j + j0))
-        pltpu.emit_pipeline(body, grid=(width // TN,), in_specs=[w, w], out_specs=[o, o, o])(WG.at[0], WU.at[0], gate0, up0, p0)
+        pltpu.emit_pipeline(body, grid=(width // TN,), in_specs=[w, w], out_specs=[o, o, o])(WG.at[0], WU.at[0], f0, e0, p0)
 
     def down():
         c = pltpu.make_async_copy(WD.at[0], wd_vm, local.at[8])
@@ -183,12 +186,15 @@
             y = dot(p_t[...], wd_vm[...]).astype(BF16)
             h = x_t[...] + y
             h_t[...] = h
-            a_vm[pl.ds(pl.multiple_of(idx.index[0] * TM, TM), TM), :] = rms(h)
-        o = pl.BlockSpec((TM, d), lambda i: (i, 0))
-        pltpu.emit_pipeline(body, grid=(tokens // TM,), in_specs=[pl.BlockSpec((TM, ff), lambda i: (i, 0)), o], out_specs=[o], _explicit_indices=True)(p0, x, h1)
-
-    def gate_up_back(at, width):
-        def body(wg_t, wu_t, wd_t, p_t, dg_t, du_t):
+            a_vm[pl.ds(pl.multiple_of(idx.index[0] * TMD, TMD), TMD), :] = rms(h)
+        o = pl.BlockSpec((TMD, d), lambda i: (i, 0))
+        pltpu.emit_pipeline(body, grid=(tokens // TMD,), in_specs=[pl.BlockSpec((TMD, ff), lambda i: (i, 0)), o], out_specs=[o], _explicit_indices=True)(p0, x, h1)
+
+    def gate_up_back(events):
+        def body(idx, wg_t, wu_t, wd_t, gd_t, dg_t, du_t):
+            for at, what in events:
+                pl.when(idx.index[0] == at)(what)
+
             @pl.loop(0, tokens // TM)
             def _(i):
                 rows = pl.ds(pl.multiple_of(i * TM, TM), TM)
@@ -198,32 +204,38 @@
                 dp = lax.dot_general(dy_vm[rows, :], wd_t[...], NT, preferred_element_type=F32).astype(BF16).astype(F32)
                 sig = jax.nn.sigmoid(g)
                 s = g * sig
-                p_t[rows, :] = (s * u).astype(BF16)
+                p_vm[rows, :] = (s * u).astype(BF16)
                 du_t[rows, :] = (dp * s).astype(BF16)
                 dg_t[rows, :] = (dp * u * (sig + s * (1 - sig))).astype(BF16)
-        j0 = at // TN
-        w = pl.BlockSpec((d, TN), lambda j: (0, j + j0))
-        o = pl.BlockSpec((tokens, TN), lambda j: (0, j + j0))
-        pltpu.emit_pipeline(body, grid=(width // TN,), in_specs=[w, w, pl.BlockSpec((TN, d), lambda j: (j + j0, 0))], out_specs=[o, o, o])(
-            WG.at[1], WU.at[1], WD.at[1], p1, dg1, du1)
+            gd_t[...] = lax.dot_general(p_vm[...], dy_vm[...], TT, preferred_element_type=F32).astype(BF16)
+        w = pl.BlockSpec((d, TN), lambda j: (0, j))
+        o = pl.BlockSpec((tokens, TN), lambda j: (0, j))
+        r = pl.BlockSpec((TN, d), lambda j: (j, 0))
+        pltpu.emit_pipeline(body, grid=(ff // TN,), in_specs=[w, w, r], out_specs=[r, o, o], _explicit_indices=True)(
+            WG.at[1], WU.at[1], WD.at[1], gd1, dg1, du1)
 
     transposed(a0T)
     for c in stores:
         c.wait()
     relay(0)
     n = len(units)
-    for u, (what, layer, at, width) in enumerate(units):
+
+    def arrive(u):
         if u + 1 < n:
             relay(u + 1)
         last(u)
         complete(u)
-        if what == "g" and layer == 0:
+
+    behind = [u for u, unit in enumerate(units) if unit[:2] == ("g", 1)]
+    for u in range(behind[0] + 1):
+        arrive(u)
+        what, layer, at, width = units[u]
+        if layer == 0 and what == "g":
             gate_up(at, width)
-        elif what == "g":
-            gate_up_back(at, width)
         elif layer == 0:
             down()
             transposed(a1T)
+    gate_up_back([(units[u][2] // TN - 2, lambda u=u: arrive(u)) for u in behind[1:]])
     for i in range(len(pieces)):
         for kind in range(9):
             go(i, kind).wait_send()
@@ -235,18 +247,17 @@
     tiles = ff // TN
     a, b = (tiles + 1) // 2 * TN, tiles // 2 * TN
     units = [("g", 0, 0, a), ("g", 0, a, b), ("d", 0, 0, 0), ("d", 1, 0, 0)]
-    at = 0
-    for k in range(4):
-        w = (tiles + 3 - k) // 4 * TN
+    at, sizes = 0, (3, 3, 4, 4)
+    while at < ff:
+        w = min((sizes[len(units) - 4] if len(units) < 8 else tiles) * TN, ff - at)
         units.append(("g", 1, at, w))
         at += w
-    assert at == ff
     count = sum(2 if u[0] == "g" else 1 for u in units)
     big = jax.ShapeDtypeStruct((tokens, ff), BF16)
     wide = jax.ShapeDtypeStruct((tokens, ff), F32)
     h = jax.ShapeDtypeStruct((tokens, d), BF16)
     hT = jax.ShapeDtypeStruct((d, tokens), BF16)
-    outs = [jax.ShapeDtypeStruct((2, d, ff), BF16)] * 2 + [jax.ShapeDtypeStruct((2, ff, d), BF16), wide, wide, big, h, hT, hT, big, big, big]
+    outs = [jax.ShapeDtypeStruct((2, d, ff), BF16)] * 2 + [jax.ShapeDtypeStruct((2, ff, d), BF16), wide, wide, big, h, hT, hT, jax.ShapeDtypeStruct((ff, d), BF16), big, big]
 
     def kernel(*refs):
         forward_kernel(units, tokens, d, ff, *refs)
@@ -257,7 +268,7 @@
         in_specs=[ANY] * 5,
         out_specs=[ANY] * len(outs),
         scratch_shapes=[
-            pltpu.VMEM((tokens, d), BF16), pltpu.VMEM((tokens, d), BF16), pltpu.VMEM((ff, d), BF16),
+            pltpu.VMEM((tokens, d), BF16), pltpu.VMEM((tokens, d), BF16), pltpu.VMEM((ff, d), BF16), pltpu.VMEM((tokens, TN), BF16),
             pltpu.VMEM(wg.shape, BF16), pltpu.VMEM(wu.shape, BF16), pltpu.VMEM(wd.shape, BF16),
             pltpu.SemaphoreType.DMA((count, 9)), pltpu.SemaphoreType.DMA((count, 9)), pltpu.SemaphoreType.DMA((9,)),
         ],
@@ -267,22 +278,23 @@
 
 
 class Unit:
-    def __init__(self, n, slot, bufs, rows, width, by_rows, outs, older, newer):
+    def __init__(self, n, slot, bufs, rows, width, by_rows, outs, older, newer, at=0):
+        self.at = at
         self.n, self.slot, self.rows, self.width, self.by_rows, self.outs, self.older, self.newer = n, slot, rows, width, by_rows, outs, older, newer
         self.G, self.Rp, self.R1, self.R2 = bufs
         self.pieces = len(outs)
         self.h = (rows if by_rows else width) // 2
 
     def block(self, b):
-        return self.G.at[:, pl.ds(pl.multiple_of(b * self.rows, 16), self.rows), pl.ds(0, self.width)]
+        return self.G.at[:, pl.ds(pl.multiple_of(b * self.rows, 16), self.rows), pl.ds(self.at, self.width)]
 
     def half(self, b, part):
         if self.by_rows:
-            return self.G.at[:, pl.ds(pl.multiple_of(b * self.rows + part * self.h, 16), self.h), :]
+            return self.G.at[:, pl.ds(pl.multiple_of(b * self.rows + part * self.h, 16), self.h), pl.ds(self.at, self.width)]
         return self.G.at[:, pl.ds(pl.multiple_of(b * self.rows, 16), self.rows), pl.ds(part * self.h, self.h)]
 
     def narrow(self, ref):
-        return ref if self.by_rows else ref.at[:, :, pl.ds(0, self.h)]
+        return ref.at[:, :, pl.ds(self.at, self.width) if self.by_rows else pl.ds(0, self.h)]
 
     def r1(self, part, which):
         return self.narrow(self.R1.at[part, which])
@@ -291,10 +303,10 @@
         return self.narrow(self.R2.at[part])
 
     def rp(self, q):
-        return self.Rp.at[q, :, :, pl.ds(0, self.width)]
-
-
-def backward_kernel(groups, tokens, d, ff, p1, dg1, du1, a1T, dy, WG, WU, WD, h1, gate0, up0, p0, a0T, gG, gU, gD,
+        return self.Rp.at[q, :, :, pl.ds(self.at, self.width)]
+
+
+def backward_kernel(groups, tokens, d, ff, gd1, dg1, du1, a1T, dy, WG, WU, WD, h1, f0, e0, p0, a0T, gG, gU, gD,
                     aT_vm, dh_vm, Gg, Rpg, R1g, R2g, Gd, Rpd, R1d, R2d, send, recv, local, credit):
     me, flip = around()
     xn, yn, pn = flip(me, 4), flip(me, 2), flip(me, 1)
@@ -311,8 +323,11 @@
 
     down_bufs = (Gd, Rpd, R1d, R2d)
     count = len(groups)
-    D = [Unit(2 * count + 1, SLOTS, down_bufs, rd, d, True, [gD.at[0]], True, False),
-         Unit(2 * count, SLOTS, down_bufs, rd, d, True, [gD.at[1]], False, True)]
+    D = {}
+    for layer in (1, 0):
+        for part, (at, width) in enumerate(((0, 512), (512, d - 512))):
+            D[layer, part] = Unit(2 * count + 2 * layer + part, SLOTS + part, down_bufs, rd, width, True,
+                                  [gD.at[layer, :, pl.ds(at, width)]], layer == 0, layer == 1, at)
     units = []
     for layer in (1, 0):
         for at, width in groups:
@@ -409,50 +424,33 @@
                     if when == at:
                         what(u)
 
-    TM = 512
+    TM = 1024
     wide_tile = pl.BlockSpec((tokens, TN), lambda j: (0, j))
     w_tile = pl.BlockSpec((d, TN), lambda j: (0, j))
 
-    def load(src, dst):
-        c = pltpu.make_async_copy(src, dst, local.at[0, 0])
-        c.start()
-        c.wait()
-
-    def down_weight(p, unit, events):
+    def down_weight(p, cols, events):
         def body(idx, p_t):
             j = idx.index[0]
             run(events, j)
-            g = lax.dot_general(p_t[...], dh_vm[...], (((0,), (0,)), ((), ())), preferred_element_type=F32)
-            unit.G[0, pl.ds(pl.multiple_of(j * TN, TN), TN), :] = g.astype(BF16)
+            g = lax.dot_general(p_t[...], dh_vm[:, cols], TT, preferred_element_type=F32)
+            Gd[0, pl.ds(pl.multiple_of(j * TN, TN), TN), cols] = g.astype(BF16)
         pltpu.emit_pipeline(body, grid=(ff // TN,), in_specs=[wide_tile], _explicit_indices=True)(p)
 
-    def store_weight(mine, j, i, g_t):
-        value = dot(aT_vm[...], g_t[...]).astype(BF16)
-        for k, u in enumerate(mine):
-            at, width = groups[k]
-
-            @pl.when((j >= at // TN) & (j < (at + width) // TN))
-            def _(u=u, at=at):
-                u.G[i, :, pl.ds(pl.multiple_of(j * TN - at, TN), TN)] = value
+    def store_weight(first, j, i, g_t):
+        per = GROUP // TN
+        slot = (j // per + first) % SLOTS
+        off = pl.multiple_of((j % per) * TN, TN)
+        Gg[slot, i, :, pl.ds(off, TN)] = dot(aT_vm[...], g_t[...]).astype(BF16)
 
     def layer1(acc, events):
-        mine = units[:count]
-
         def body(idx, dg_t, du_t, wg_t, wu_t):
             j = idx.index[0]
             run(events, j)
-            store_weight(mine, j, 0, dg_t)
-            store_weight(mine, j, 1, du_t)
-
-            def both(i):
-                rows = pl.ds(pl.multiple_of(i * TM, TM), TM)
-                return rows, lax.dot_general(dg_t[rows, :], wg_t[...], NT, preferred_element_type=F32) + lax.dot_general(
-                    du_t[rows, :], wu_t[...], NT, preferred_element_type=F32)
-
-            @pl.loop(0, tokens // TM)
-            def _(i):
-                rows, value = both(i)
-                acc[rows, :] = jnp.where(j == 0, value, acc[rows, :] + value)
+            store_weight(0, j, 0, dg_t)
+            store_weight(0, j, 1, du_t)
+            value = lax.dot_general(dg_t[...], wg_t[...], NT, preferred_element_type=F32) + lax.dot_general(
+                du_t[...], wu_t[...], NT, preferred_element_type=F32)
+            acc[...] = jnp.where(j == 0, value, acc[...] + value)
         pltpu.emit_pipeline(body, grid=(ff // TN,), in_specs=[wide_tile, wide_tile, w_tile, w_tile], _explicit_indices=True)(dg1, du1, WG.at[1], WU.at[1])
 
         def norm(idx, h_t):
@@ -465,9 +463,7 @@
         pltpu.emit_pipeline(norm, grid=(tokens // TN,), in_specs=[pl.BlockSpec((TN, d), lambda i: (i, 0))], _explicit_indices=True)(h1)
 
     def layer0(dg_vm, du_vm, events):
-        mine = units[count:]
-
-        def body(idx, wd_t, gate_t, up_t):
+        def body(idx, wd_t, f_t, e_t):
             j = idx.index[0]
             run(events, j)
 
@@ -475,63 +471,69 @@
             def _(i):
                 rows = pl.ds(pl.multiple_of(i * TM, TM), TM)
                 dp = lax.dot_general(dh_vm[rows, :], wd_t[...], NT, preferred_element_type=F32).astype(BF16).astype(F32)
-                g = gate_t[rows, :]
-                sig = jax.nn.sigmoid(g)
-                s = g * sig
-                du_vm[rows, :] = (dp * s).astype(BF16)
-                dg_vm[rows, :] = (dp * up_t[rows, :] * (sig + s * (1 - sig))).astype(BF16)
-            store_weight(mine, j, 0, dg_vm)
-            store_weight(mine, j, 1, du_vm)
+                du_vm[rows, :] = (dp * f_t[rows, :]).astype(BF16)
+                dg_vm[rows, :] = (dp * e_t[rows, :]).astype(BF16)
+            store_weight(count, j, 0, dg_vm)
+            store_weight(count, j, 1, du_vm)
         pltpu.emit_pipeline(body, grid=(ff // TN,), in_specs=[pl.BlockSpec((TN, d), lambda j: (j, 0)), wide_tile, wide_tile], _explicit_indices=True)(
-            WD.at[0], gate0, up0)
+            WD.at[0], f0, e0)
 
     tiles = ff // TN
-    order = {"D1": [], "L1": [], "D0": [], "L0": [], "end": []}
+    order = {"L1": [], "Da": [], "Db": [], "L0": [], "end": []}
+    LATER = 7
 
     def spot(tick):
-        if tick < tiles:
-            return "L1", tick
-        tick -= tiles
-        if tick < 5:
-            return "D0", 4 * tick
-        tick -= 5
-        return ("L0", tick) if tick < tiles else ("end", tick)
+        for name, ticks, step in (("L1", tiles, 1), ("Da", 4, 5), ("Db", 3, 6), ("L0", tiles, 1)):
+            if tick < ticks:
+                return name, tick * step
+            tick -= ticks
+        return "end", tick
 
     def plan(u, ticks):
         for tick, what in zip(ticks, (s0, s1, s2, s3, s4)):
-            where, at = spot(tick)
-            order[where].append((at, what, u))
-
-    plan(D[1], (0, 2, 9, 12, 14))
+            if tick is not None:
+                where, at = spot(tick)
+                order[where].append((at, what, u))
+
+    plan(D[1, 0], (None, 1, 5, 8, 10))
+    plan(D[1, 1], (2, 10, 14, 17, 19))
     for k, u in enumerate(units):
         at, width = groups[k % count]
-        end = (at + width) // TN + (0 if k < count else tiles + 5)
-        plan(u, (end, end + 1, end + 5, end + 7, end + 8))
-    start = tiles + 5
-    plan(D[0], (start, start + 2, start + 9, start + 12, start + 14))
+        end = (at + width) // TN + (0 if k < count else tiles + LATER)
+        plan(u, (end, end + 1, end + 5, end + 8, end + 9))
+    start = tiles + 4
+    plan(D[0, 0], (start, start + 1, start + 5, start + 8, start + 10))
+    plan(D[0, 1], (start + 3, start + 4, start + 8, start + 11, start + 13))
     for events in order.values():
         events.sort(key=lambda e: (e[0], -(s0, s1, s2, s3, s4).index(e[1])))
 
-    load(dy, dh_vm)
-    load(a1T, aT_vm)
-    down_weight(p1, D[1], [])
+    copies = [pltpu.make_async_copy(src, dst, local.at[0, k]) for k, (src, dst) in enumerate(((gd1, Gd.at[0]), (dy, dh_vm), (a1T, aT_vm)))]
+    for c in copies:
+        c.start()
+    copies[0].wait()
+    s0(D[1, 0])
+    for c in copies[1:]:
+        c.wait()
     pl.run_scoped(lambda acc: layer1(acc, order["L1"]), pltpu.VMEM((tokens, d), F32))
-    load(a0T, aT_vm)
-    down_weight(p0, D[0], order["D0"])
+    c = pltpu.make_async_copy(a0T, aT_vm, local.at[0, 2])
+    c.start()
+    down_weight(p0, slice(0, 512), order["Da"])
+    down_weight(p0, slice(512, d), order["Db"])
+    c.wait()
     pl.run_scoped(lambda a, b: layer0(a, b, order["L0"]), pltpu.VMEM((tokens, TN), BF16), pltpu.VMEM((tokens, TN), BF16))
     for _, what, u in order["end"]:
         what(u)
 
 
-def backward(p1, dg1, du1, a1T, dy, WG, WU, WD, h1, gate0, up0, p0, a0T):
+def backward(gd1, dg1, du1, a1T, dy, WG, WU, WD, h1, f0, e0, p0, a0T):
     tokens, d = dy.shape
     ff = dg1.shape[1]
     tiles, groups, at = ff // TN, [], 0
     while at < ff:
-        width = min(4 * TN, ff - at)
+        width = min(GROUP, ff - at)
         groups.append((at, width))
         at += width
-    C, rg, rd, slots, n = 4 * TN, d // 8, ff // 8, 3, 2 * len(groups) + 2
+    C, rg, rd, slots, n = GROUP, d // 8, ff // 8, 4, 2 * len(groups) + 4
     outs = [jax.ShapeDtypeStruct((2, rg, ff), BF16)] * 2 + [jax.ShapeDtypeStruct((2, rd, d), BF16)]
 
     def kernel(*refs):
@@ -548,12 +550,12 @@
             pltpu.VMEM((slots, 2, 2, 2, rg, C // 2), BF16), pltpu.VMEM((slots, 2, 2, rg, C // 2), BF16),
             pltpu.VMEM((1, ff, d), BF16), pltpu.VMEM((4, 1, rd, d), BF16),
             pltpu.VMEM((2, 2, 1, rd // 2, d), BF16), pltpu.VMEM((2, 1, rd // 2, d), BF16),
-            pltpu.SemaphoreType.DMA((n, 10)), pltpu.SemaphoreType.DMA((n, 10)), pltpu.SemaphoreType.DMA((n, 2)),
-            pltpu.SemaphoreType.REGULAR((slots + 1, 3)),
+            pltpu.SemaphoreType.DMA((n, 10)), pltpu.SemaphoreType.DMA((n, 10)), pltpu.SemaphoreType.DMA((n, 3)),
+            pltpu.SemaphoreType.REGULAR((slots + 2, 3)),
         ],
         compiler_params=pltpu.CompilerParams(collective_id=1, has_side_effects=True, vmem_limit_bytes=67000000),
         name="backward",
-    )(p1, dg1, du1, a1T, dy, WG, WU, WD, h1, gate0, up0, p0, a0T)
+    )(gd1, dg1, du1, a1T, dy, WG, WU, WD, h1, f0, e0, p0, a0T)
 
 
 def adamw(w, m, v, g):
@@ -567,8 +569,8 @@
     def step(x, dy, *arrays):
         weights, m, v = (arrays[i : i + 3] for i in (0, 3, 6))
         x, dy = x[0], dy[0]
-        WG, WU, WD, gate0, up0, p0, h1, a0T, a1T, p1, dg1, du1 = forward(x, dy, *weights)
-        gradients = [g.astype(F32) for g in backward(p1, dg1, du1, a1T, dy, WG, WU, WD, h1, gate0, up0, p0, a0T)]
+        WG, WU, WD, f0, e0, p0, h1, a0T, a1T, gd1, dg1, du1 = forward(x, dy, *weights)
+        gradients = [g.astype(F32) for g in backward(gd1, dg1, du1, a1T, dy, WG, WU, WD, h1, f0, e0, p0, a0T)]
         new = [adamw(w.astype(F32), m, v, g) for w, m, v, g in zip(weights, m, v, gradients, strict=True)]
         return tuple(one[which] for which in range(3) for one in new)
 

time: 685 us -> 583 us (0.85)
  Pallas kernels: 657 us -> 555 us
    pallas_call x1, Pallas kernels: 372 us -> 261 us  [backward(): pl.pallas_call(kernel, out_shape=outs, in_specs=[ANY] * 13, out_specs=[AN...]
    pallas_call x1, Pallas kernels: 285 us -> 294 us  [forward(): pl.pallas_call(kernel, out_shape=outs, in_specs=[ANY] * 5, out_specs=[ANY...]
where the time goes in v3:
time: 583 us; the launch traced here: 582 us
  Pallas kernels  555 us (95%)
  other arithmetic  24.2 us (4%)
    pallas_call x1, Pallas kernels, forward(): pl.pallas_call(kernel, out_shape=outs, in_specs=[ANY] * 5, out_specs=[ANY...  294 us
    pallas_call x1, Pallas kernels, backward(): pl.pallas_call(kernel, out_shape=outs, in_specs=[ANY] * 13, out_specs=[AN...  261 us
    convert_element_type x2, other arithmetic, adamw(): return ((w - 0.02 * step).astype(BF16), m, v)  24.2 us

profile of v3, /device:TPU:0, one launch (start us, length us, event | category | flops | bytes accessed | tf_op | source)
XLA Modules:
  0.0 581.6 jit_solution(17655945484588906388)
XLA Ops:
  0.6 294.2 %forward.1 = (bf16[2,896,4864]{2,1,0:T(8,128)(2,1)}, bf16[2,896,4864]{2,1,0:T(8,128)(2,1)}, bf16[2,4864,896]{2,1,0:T(8,128)(2,1)}, f32[2048,4864]{1,0:T(8,128)},...) custom-call(bf16[2048,896]{1,0:T(8,128)(2,1)} %bitcast.4, ...), custom_call_target="tpu_custom_call" | custom-call | tf_op jit(solution)/shard_map/forward/pallas_call | solution.py:265
  294.9 261.0 %backward.1 = (bf16[2,112,4864]{2,1,0:T(8,128)(2,1)}, bf16[2,112,4864]{2,1,0:T(8,128)(2,1)}, bf16[2,608,896]{2,1,0:T(8,128)(2,1)}) custom-call(bf16[4864,896]{1,0:T(8,128)(2,1)} %get-tuple-element.24.refs_0_, bf16[2048,4864]{1,0:T(8,128)(2,1)} %get-tuple-element.25.refs_1_, bf16[2048,4864]{1,0:T(8,128)(2,1)} %get-tuple-element.26.refs_2_, ...), custom_call_target="tpu_custom_call" | custom-call | tf_op jit(solution)/shard_map/backward/pallas_call | solution.py:542
  556.0 0.0 copy-start
  556.0 0.0 copy-start.1
  556.0 0.0 copy-start.2
  556.0 9.2 %fusion.10 = (bf16[2,608,896]{2,1,0:T(8,128)(2,1)}, f32[2,608,896]{2,1,0:T(8,128)}, f32[2,608,896]{2,1,0:T(8,128)}) fusion(bf16[2,608,896]{2,1,0:T(8,128)(2,1)} %refs_4_.1, bf16[2,608,896]{2,1,0:T(8,128)(2,1)} %get-tuple-element.38, f32[2,608,896]{2,1,0:T(8,128)} %param.21, f32[2,608,896]{2,1,0:T(8,128)} %param.18), kind=kLoop, calls=%fused_computation.22 | loop fusion | flops 17432576 | bytes 23969792 | tf_op jit(solution)/shard_map/convert_element_type | solution.py:565
  565.2 0.0 copy-done
  565.2 0.2 copy-done.1
  565.3 1.2 copy-done.2
  566.6 15.1 %fusion.2 = (bf16[2,112,4864]{2,1,0:T(8,128)(2,1)}, f32[2,112,4864]{2,1,0:T(8,128)}, f32[2,112,4864]{2,1,0:T(8,128)}, bf16[2,112,4864]{2,1,0:T(8,128)(2,1)}, f32...) fusion(bf16[2,112,4864]{2,1,0:T(8,128)(2,1)S(1)} %copy-done, bf16[2,112,4864]{2,1,0:T(8,128)(2,1)S(1)} %copy-done.2, ...), kind=kLoop, calls=%fused_computation.14 | loop fusion | flops 34865152 | bytes 47939584 | tf_op jit(solution)/shard_map/convert_element_type | solution.py:565
Async XLA Ops:
  556.0 9.2 %copy-start = (bf16[2,112,4864]{2,1,0:T(8,128)(2,1)S(1)}, bf16[2,112,4864]{2,1,0:T(8,128)(2,1)}, u32[]{:S(2)}) copy-start(bf16[2,112,4864]{2,1,0:T(8,128)(2,1)} %refs_2_.1) | copy-start | bytes 6537220
  556.0 9.4 %copy-start.1 = (bf16[2,112,4864]{2,1,0:T(8,128)(2,1)S(1)}, bf16[2,112,4864]{2,1,0:T(8,128)(2,1)}, u32[]{:S(2)}) copy-start(bf16[2,112,4864]{2,1,0:T(8,128)(2,1)} %refs_3_.1) | copy-start | bytes 6537220
  556.0 10.6 %copy-start.2 = (bf16[2,112,4864]{2,1,0:T(8,128)(2,1)S(1)}, bf16[2,112,4864]{2,1,0:T(8,128)(2,1)}, u32[]{:S(2)}) copy-start(bf16[2,112,4864]{2,1,0:T(8,128)(2,1)} %get-tuple-element.36) | copy-start | bytes 6537220

commit v4 on v3

--- a/solution.py
+++ b/solution.py
@@ -52,7 +52,7 @@
         return self.full.at[self.layer, pl.ds(pl.multiple_of(owner * self.rows + off, 16), n), cols]
 
 
-def forward_kernel(units, tokens, d, ff, x, dy, wg, wu, wd, WG, WU, WD, f0, e0, p0, h1, a0T, a1T, gd1, dg1, du1,
+def forward_kernel(units, tokens, d, ff, x, dy, wg, wu, wd, WG, WU, WD, f0, e0, p0, h1, a0, a1, gd1, dg1, du1,
                    a_vm, dy_vm, wd_vm, p_vm, own_g, own_u, own_d, send, recv, local):
     me, flip = around()
     xn, yn, pn = flip(me, 4), flip(me, 2), flip(me, 1)
@@ -149,19 +149,11 @@
         c.start()
         stores.append(c)
 
-    def transpose_out(j, out):
-        out[...] = a_vm[pl.ds(pl.multiple_of(j * TN, TN), TN), :].T
-
-    def transposed(aT):
-        def body(idx, out):
-            transpose_out(idx.index[0], out)
-        pltpu.emit_pipeline(body, grid=(tokens // TN,), out_specs=[pl.BlockSpec((d, TN), lambda j: (0, j))], _explicit_indices=True)(aT)
-
     TM, TMD = 1024, 512
 
     def gate_up(at, width):
         def body(wg_t, wu_t, f_t, e_t, p_t):
-            @pl.loop(0, tokens // TM)
+            @pl.loop(0, tokens // TM, unroll=True)
             def _(i):
                 rows = pl.ds(pl.multiple_of(i * TM, TM), TM)
                 a = a_vm[rows, :]
@@ -178,7 +170,7 @@
         pltpu.emit_pipeline(body, grid=(width // TN,), in_specs=[w, w], out_specs=[o, o, o])(WG.at[0], WU.at[0], f0, e0, p0)
 
     def down():
-        c = pltpu.make_async_copy(WD.at[0], wd_vm, local.at[8])
+        c = pltpu.make_async_copy(WD.at[0], wd_vm, local.at[10])
         c.start()
         c.wait()
 
@@ -195,7 +187,7 @@
             for at, what in events:
                 pl.when(idx.index[0] == at)(what)
 
-            @pl.loop(0, tokens // TM)
+            @pl.loop(0, tokens // TM, unroll=True)
             def _(i):
                 rows = pl.ds(pl.multiple_of(i * TM, TM), TM)
                 a = a_vm[rows, :]
@@ -214,7 +206,8 @@
         pltpu.emit_pipeline(body, grid=(ff // TN,), in_specs=[w, w, r], out_specs=[r, o, o], _explicit_indices=True)(
             WG.at[1], WU.at[1], WD.at[1], gd1, dg1, du1)
 
-    transposed(a0T)
+    keep = [pltpu.make_async_copy(a_vm, a, local.at[8 + k]) for k, a in enumerate((a0, a1))]
+    keep[0].start()
     for c in stores:
         c.wait()
     relay(0)
@@ -233,9 +226,11 @@
         if layer == 0 and what == "g":
             gate_up(at, width)
         elif layer == 0:
+            keep[0].wait()
             down()
-            transposed(a1T)
+            keep[1].start()
     gate_up_back([(units[u][2] // TN - 2, lambda u=u: arrive(u)) for u in behind[1:]])
+    keep[1].wait()
     for i in range(len(pieces)):
         for kind in range(9):
             go(i, kind).wait_send()
@@ -256,8 +251,7 @@
     big = jax.ShapeDtypeStruct((tokens, ff), BF16)
     wide = jax.ShapeDtypeStruct((tokens, ff), F32)
     h = jax.ShapeDtypeStruct((tokens, d), BF16)
-    hT = jax.ShapeDtypeStruct((d, tokens), BF16)
-    outs = [jax.ShapeDtypeStruct((2, d, ff), BF16)] * 2 + [jax.ShapeDtypeStruct((2, ff, d), BF16), wide, wide, big, h, hT, hT, jax.ShapeDtypeStruct((ff, d), BF16), big, big]
+    outs = [jax.ShapeDtypeStruct((2, d, ff), BF16)] * 2 + [jax.ShapeDtypeStruct((2, ff, d), BF16), wide, wide, big, h, h, h, jax.ShapeDtypeStruct((ff, d), BF16), big, big]
 
     def kernel(*refs):
         forward_kernel(units, tokens, d, ff, *refs)
@@ -270,7 +264,7 @@
         scratch_shapes=[
             pltpu.VMEM((tokens, d), BF16), pltpu.VMEM((tokens, d), BF16), pltpu.VMEM((ff, d), BF16), pltpu.VMEM((tokens, TN), BF16),
             pltpu.VMEM(wg.shape, BF16), pltpu.VMEM(wu.shape, BF16), pltpu.VMEM(wd.shape, BF16),
-            pltpu.SemaphoreType.DMA((count, 9)), pltpu.SemaphoreType.DMA((count, 9)), pltpu.SemaphoreType.DMA((9,)),
+            pltpu.SemaphoreType.DMA((count, 9)), pltpu.SemaphoreType.DMA((count, 9)), pltpu.SemaphoreType.DMA((11,)),
         ],
         compiler_params=pltpu.CompilerParams(collective_id=0, has_side_effects=True, vmem_limit_bytes=60 * 2**20),
         name="forward",
@@ -306,8 +300,8 @@
         return self.Rp.at[q, :, :, pl.ds(self.at, self.width)]
 
 
-def backward_kernel(groups, tokens, d, ff, gd1, dg1, du1, a1T, dy, WG, WU, WD, h1, f0, e0, p0, a0T, gG, gU, gD,
-                    aT_vm, dh_vm, Gg, Rpg, R1g, R2g, Gd, Rpd, R1d, R2d, send, recv, local, credit):
+def backward_kernel(groups, tokens, d, ff, gd1, dg1, du1, a1, dy, WG, WU, WD, h1, f0, e0, p0, a0, gG, gU, gD,
+                    a_vm, dh_vm, Gg, Rpg, R1g, R2g, Gd, Rpd, R1d, R2d, send, recv, local, credit):
     me, flip = around()
     xn, yn, pn = flip(me, 4), flip(me, 2), flip(me, 1)
     core, q0 = me % 2, me // 2
@@ -440,7 +434,7 @@
         per = GROUP // TN
         slot = (j // per + first) % SLOTS
         off = pl.multiple_of((j % per) * TN, TN)
-        Gg[slot, i, :, pl.ds(off, TN)] = dot(aT_vm[...], g_t[...]).astype(BF16)
+        Gg[slot, i, :, pl.ds(off, TN)] = lax.dot_general(a_vm[...], g_t[...], TT, preferred_element_type=F32).astype(BF16)
 
     def layer1(acc, events):
         def body(idx, dg_t, du_t, wg_t, wu_t):
@@ -467,7 +461,7 @@
             j = idx.index[0]
             run(events, j)
 
-            @pl.loop(0, tokens // TM)
+            @pl.loop(0, tokens // TM, unroll=True)
             def _(i):
                 rows = pl.ds(pl.multiple_of(i * TM, TM), TM)
                 dp = lax.dot_general(dh_vm[rows, :], wd_t[...], NT, preferred_element_type=F32).astype(BF16).astype(F32)
@@ -507,7 +501,7 @@
     for events in order.values():
         events.sort(key=lambda e: (e[0], -(s0, s1, s2, s3, s4).index(e[1])))
 
-    copies = [pltpu.make_async_copy(src, dst, local.at[0, k]) for k, (src, dst) in enumerate(((gd1, Gd.at[0]), (dy, dh_vm), (a1T, aT_vm)))]
+    copies = [pltpu.make_async_copy(src, dst, local.at[0, k]) for k, (src, dst) in enumerate(((gd1, Gd.at[0]), (dy, dh_vm), (a1, a_vm)))]
     for c in copies:
         c.start()
     copies[0].wait()
@@ -515,7 +509,7 @@
     for c in copies[1:]:
         c.wait()
     pl.run_scoped(lambda acc: layer1(acc, order["L1"]), pltpu.VMEM((tokens, d), F32))
-    c = pltpu.make_async_copy(a0T, aT_vm, local.at[0, 2])
+    c = pltpu.make_async_copy(a0, a_vm, local.at[0, 2])
     c.start()
     down_weight(p0, slice(0, 512), order["Da"])
     down_weight(p0, slice(512, d), order["Db"])
@@ -525,7 +519,7 @@
         what(u)
 
 
-def backward(gd1, dg1, du1, a1T, dy, WG, WU, WD, h1, f0, e0, p0, a0T):
+def backward(gd1, dg1, du1, a1, dy, WG, WU, WD, h1, f0, e0, p0, a0):
     tokens, d = dy.shape
     ff = dg1.shape[1]
     tiles, groups, at = ff // TN, [], 0
@@ -545,7 +539,7 @@
         in_specs=[ANY] * 13,
         out_specs=[ANY] * 3,
         scratch_shapes=[
-            pltpu.VMEM((d, tokens), BF16), pltpu.VMEM((tokens, d), BF16),
+            pltpu.VMEM((tokens, d), BF16), pltpu.VMEM((tokens, d), BF16),
             pltpu.VMEM((slots, 2, d, C), BF16), pltpu.VMEM((slots, 4, 2, rg, C), BF16),
             pltpu.VMEM((slots, 2, 2, 2, rg, C // 2), BF16), pltpu.VMEM((slots, 2, 2, rg, C // 2), BF16),
             pltpu.VMEM((1, ff, d), BF16), pltpu.VMEM((4, 1, rd, d), BF16),
@@ -555,7 +549,7 @@
         ],
         compiler_params=pltpu.CompilerParams(collective_id=1, has_side_effects=True, vmem_limit_bytes=67000000),
         name="backward",
-    )(gd1, dg1, du1, a1T, dy, WG, WU, WD, h1, f0, e0, p0, a0T)
+    )(gd1, dg1, du1, a1, dy, WG, WU, WD, h1, f0, e0, p0, a0)
 
 
 def adamw(w, m, v, g):
@@ -569,8 +563,8 @@
     def step(x, dy, *arrays):
         weights, m, v = (arrays[i : i + 3] for i in (0, 3, 6))
         x, dy = x[0], dy[0]
-        WG, WU, WD, f0, e0, p0, h1, a0T, a1T, gd1, dg1, du1 = forward(x, dy, *weights)
-        gradients = [g.astype(F32) for g in backward(gd1, dg1, du1, a1T, dy, WG, WU, WD, h1, f0, e0, p0, a0T)]
+        WG, WU, WD, f0, e0, p0, h1, a0, a1, gd1, dg1, du1 = forward(x, dy, *weights)
+        gradients = [g.astype(F32) for g in backward(gd1, dg1, du1, a1, dy, WG, WU, WD, h1, f0, e0, p0, a0)]
         new = [adamw(w.astype(F32), m, v, g) for w, m, v, g in zip(weights, m, v, gradients, strict=True)]
         return tuple(one[which] for which in range(3) for one in new)
 

time: 583 us -> 571 us (0.979)
  Pallas kernels: 555 us -> 544 us
    pallas_call x1, Pallas kernels: 294 us -> 283 us  [forward(): pl.pallas_call(kernel, out_shape=outs, in_specs=[ANY] * 5, out_specs=[ANY...]
where the time goes in v4:
time: 571 us; the launch traced here: 570 us
  Pallas kernels  544 us (95%)
  other arithmetic  24.2 us (4%)
    pallas_call x1, Pallas kernels, forward(): pl.pallas_call(kernel, out_shape=outs, in_specs=[ANY] * 5, out_specs=[ANY...  283 us
    pallas_call x1, Pallas kernels, backward(): pl.pallas_call(kernel, out_shape=outs, in_specs=[ANY] * 13, out_specs=[AN...  261 us
    convert_element_type x2, other arithmetic, adamw(): return ((w - 0.02 * step).astype(BF16), m, v)  24.2 us

profile of v4, /device:TPU:0, one launch (start us, length us, event | category | flops | bytes accessed | tf_op | source)
XLA Modules:
  0.0 570.2 jit_solution(2344708789508189538)
XLA Ops:
  0.6 283.2 %forward.1 = (bf16[2,896,4864]{2,1,0:T(8,128)(2,1)}, bf16[2,896,4864]{2,1,0:T(8,128)(2,1)}, bf16[2,4864,896]{2,1,0:T(8,128)(2,1)}, f32[2048,4864]{1,0:T(8,128)},...) custom-call(bf16[2048,896]{1,0:T(8,128)(2,1)} %bitcast.4, ...), custom_call_target="tpu_custom_call" | custom-call | tf_op jit(solution)/shard_map/forward/pallas_call | solution.py:259
  283.8 260.8 %backward.1 = (bf16[2,112,4864]{2,1,0:T(8,128)(2,1)}, bf16[2,112,4864]{2,1,0:T(8,128)(2,1)}, bf16[2,608,896]{2,1,0:T(8,128)(2,1)}) custom-call(bf16[4864,896]{1,0:T(8,128)(2,1)} %get-tuple-element.24.refs_0_, bf16[2048,4864]{1,0:T(8,128)(2,1)} %get-tuple-element.25.refs_1_, bf16[2048,4864]{1,0:T(8,128)(2,1)} %get-tuple-element.26.refs_2_, ...), custom_call_target="tpu_custom_call" | custom-call | tf_op jit(solution)/shard_map/backward/pallas_call | solution.py:536
  544.6 0.0 copy-start
  544.6 0.0 copy-start.1
  544.6 0.0 copy-start.2
  544.6 9.2 %fusion.10 = (bf16[2,608,896]{2,1,0:T(8,128)(2,1)}, f32[2,608,896]{2,1,0:T(8,128)}, f32[2,608,896]{2,1,0:T(8,128)}) fusion(bf16[2,608,896]{2,1,0:T(8,128)(2,1)} %refs_4_.1, bf16[2,608,896]{2,1,0:T(8,128)(2,1)} %get-tuple-element.38, f32[2,608,896]{2,1,0:T(8,128)} %param.21, f32[2,608,896]{2,1,0:T(8,128)} %param.18), kind=kLoop, calls=%fused_computation.22 | loop fusion | flops 17432576 | bytes 23969792 | tf_op jit(solution)/shard_map/convert_element_type | solution.py:559
  553.8 0.0 copy-done
  553.8 0.2 copy-done.1
  554.0 1.2 copy-done.2
  555.2 15.1 %fusion.2 = (bf16[2,112,4864]{2,1,0:T(8,128)(2,1)}, f32[2,112,4864]{2,1,0:T(8,128)}, f32[2,112,4864]{2,1,0:T(8,128)}, bf16[2,112,4864]{2,1,0:T(8,128)(2,1)}, f32...) fusion(bf16[2,112,4864]{2,1,0:T(8,128)(2,1)S(1)} %copy-done, bf16[2,112,4864]{2,1,0:T(8,128)(2,1)S(1)} %copy-done.2, ...), kind=kLoop, calls=%fused_computation.14 | loop fusion | flops 34865152 | bytes 47939584 | tf_op jit(solution)/shard_map/convert_element_type | solution.py:559
Async XLA Ops:
  544.6 9.2 %copy-start = (bf16[2,112,4864]{2,1,0:T(8,128)(2,1)S(1)}, bf16[2,112,4864]{2,1,0:T(8,128)(2,1)}, u32[]{:S(2)}) copy-start(bf16[2,112,4864]{2,1,0:T(8,128)(2,1)} %refs_2_.1) | copy-start | bytes 6537220
  544.6 9.4 %copy-start.1 = (bf16[2,112,4864]{2,1,0:T(8,128)(2,1)S(1)}, bf16[2,112,4864]{2,1,0:T(8,128)(2,1)}, u32[]{:S(2)}) copy-start(bf16[2,112,4864]{2,1,0:T(8,128)(2,1)} %refs_3_.1) | copy-start | bytes 6537220
  544.6 10.6 %copy-start.2 = (bf16[2,112,4864]{2,1,0:T(8,128)(2,1)S(1)}, bf16[2,112,4864]{2,1,0:T(8,128)(2,1)}, u32[]{:S(2)}) copy-start(bf16[2,112,4864]{2,1,0:T(8,128)(2,1)} %get-tuple-element.36) | copy-start | bytes 6537220
